TPU v7x, 128 devices: a whole 4x4x4 slice. The times are simulated.
128 devices in a mesh: row: 8 (over z, y_hi), col: 16 (over x, y_lo, core).
Axes of the slice: x: 4, y: 4 (y_hi: 2, y_lo: 2; y = y_hi * 2 + y_lo), z: 4, core: 2. Of those that a mesh axis runs over, the one named last changes fastest.
Arguments:
- tri_panels: float32 [8192, 8192], P('row', 'col'), may hold values from -1 to 2, as said below
- rhs_rows: float32 [8192, 2048], P(('row', 'col')), may hold values from -6 to 6
Outputs:
- rhs_grid: float32 [8192, 2048], P('row', 'col')
Inputs may be any that keep to these rules, and one draw needn't show every extreme that they name: `tri_panels`: in L's row order the entries above the diagonal are zero and the diagonal entries are positive.
All inputs are finite; a program needn't handle non-finite values.
Results may differ from a plain program's by a relative error of at most 0.00011.
Values sent between devices are 32-bit elements; how exact they have to be, the bound alone decides.
No kernel may reach another device: no remote copies, remote signals or barrier semaphores. Data moves between devices by JAX's collectives and lax.ppermute only.
A program may use at most 256 MiB of HBM per device.

v0:
```python
import jax
import jax.numpy as jnp
from jax import lax
from jax.sharding import PartitionSpec as P


def picked(array, axis, root):
    return lax.dynamic_index_in_dim(lax.all_gather(array, axis), root, 0, keepdims=False)


def on_device(tri_panels, rhs_rows):
    row_count = lax.axis_size("row")
    col_count = lax.axis_size("col")
    row_position = lax.axis_index("row")
    col_position = lax.axis_index("col")
    local_rows, block_size = tri_panels.shape
    blocks = local_rows // block_size
    sub_rows = block_size // col_count
    parted = rhs_rows.reshape(blocks, sub_rows, rhs_rows.shape[1])
    state_rhs = lax.all_to_all(parted, "col", split_axis=2, concat_axis=1, tiled=True)
    identity_block = jnp.eye(block_size, dtype=jnp.float32)
    own_pieces = tri_panels.reshape(blocks, block_size, block_size)
    own_diag = lax.dynamic_index_in_dim(own_pieces, col_position // row_count, 0, keepdims=False)
    own_diag = jnp.where(col_position % row_count == row_position, own_diag, identity_block)
    own_inverse = jax.scipy.linalg.solve_triangular(own_diag, identity_block, lower=True)

    def advance(state_rhs, panel_cols, inverse_block, step_index, first_slot):
        count = blocks - first_slot
        owner_row = step_index % row_count
        slot_index = step_index // row_count
        pieces = panel_cols.reshape(count, block_size, block_size)
        current = lax.dynamic_index_in_dim(state_rhs, slot_index, 0, keepdims=False)
        local_solution = jnp.dot(
            inverse_block,
            current,
            precision=lax.Precision.HIGHEST,
            preferred_element_type=jnp.float32,
        )
        solution = picked(local_solution, "row", owner_row)
        stored = jnp.where(row_position == owner_row, solution, current)
        state_rhs = lax.dynamic_update_index_in_dim(state_rhs, stored, slot_index, 0)
        global_block = (first_slot + jnp.arange(count, dtype=jnp.int32)) * row_count + row_position
        product = jnp.einsum("sij,jc->sic", pieces, solution, precision=lax.Precision.HIGHEST)
        trailing = state_rhs[first_slot:]
        trailing = jnp.where(
            (global_block > step_index)[:, None, None], trailing - product, trailing
        )
        if first_slot > 0:
            return jnp.concatenate([state_rhs[:first_slot], trailing], 0)
        return trailing

    group_count = (col_count + row_count - 1) // row_count
    everything, inverses = (
        lax.all_gather(tri_panels, "col", axis=1, tiled=True),
        lax.all_gather(own_inverse, "col", axis=1, tiled=True),
    )
    for first_slot in range(group_count):
        begin_step = first_slot * row_count
        end_step = min(begin_step + row_count, col_count)
        own_rows = everything[first_slot * block_size :]

        def upfront_step(step_index, state_rhs, own_rows=own_rows, first_slot=first_slot):
            panel_cols = lax.dynamic_slice_in_dim(own_rows, step_index * block_size, block_size, 1)
            inverse_block = lax.dynamic_slice_in_dim(
                inverses, step_index * block_size, block_size, 1
            )
            return advance(state_rhs, panel_cols, inverse_block, step_index, first_slot)

        state_rhs = lax.fori_loop(begin_step, end_step, upfront_step, state_rhs)
    return state_rhs.reshape(local_rows, state_rhs.shape[2])


def solution(mesh):
    return jax.shard_map(
        on_device,
        mesh=mesh,
        in_specs=(P("row", "col"), P(("row", "col"), None)),
        out_specs=P("row", "col"),
        check_vma=False,
    )
```

profile of v0, /device:TPU:120, one launch (start us, length us, event | category | flops | bytes accessed | tf_op | source)
XLA Modules:
  0.0 1220.5 jit_solution(3915089604845928567)
XLA Ops:
  9.3 11.6 while.33
  20.9 39.3 %custom-call.4 = f32[4,128,128]{1,2,0:T(8,128)S(1)} custom-call(f32[4,128,128]{2,1,0:T(8,128)S(1)} %get-tuple-element.290), custom_call_target="InvertDiagBlocksLowerTriangular" | custom-call | tf_op jit(solution)/shard_map/jit(_solve_triangular)/triangular_solve | solution.py:25
  71.1 5.8 all-to-all-start
  76.9 15.4 %all-to-all-done = f32[16,1,8192]{2,1,0:T(1,128)S(1)} async-done(((f32[16,1,8192]{2,1,0:T(1,128)}), f32[16,1,8192]{2,1,0:T(1,128)S(1)}, u32[]{:S(2)}, u32[]{:S(2)}) %all-to-all-start) | async-done | bytes 524320 | tf_op jit(solution)/shard_map/all_to_all | solution.py:20
  97.3 88.9 %all-gather.13.cloned.1.call-done = f32[1024,8192]{1,0:T(8,128)} async-done(((f32[1024,512]{1,0:T(8,128)}), f32[1024,8192]{1,0:T(8,128)}) %all-gather.13.cloned.1.call-update) | async-done | bytes 33554448 | tf_op jit(solution)/shard_map/all_gather | solution.py:54
  186.2 11.5 slice.70
  197.7 82.4 %all-gather.11.cloned.1.call-done = f32[512,8192]{1,0:T(8,128)} async-done(((f32[512,512]{1,0:T(8,128)}), f32[512,8192]{1,0:T(8,128)}) %all-gather.11.cloned.1.call-update) | async-done | bytes 16777232 | tf_op jit(solution)/shard_map/all_gather | solution.py:55
  280.1 468.8 %while.31 = (s32[]{:T(128)}, f32[2,512,128]{2,1,0:T(8,128)S(1)}, s32[]{:T(128)}, f32[512,8192]{1,0:T(8,128)}, f32[1024,8192]{1,0:T(8,128)}, /*index=5*/s32[]{:T(...) while((s32[]{:T(128)}, f32[2,512,128]{2,1,0:T(8,128)S(1)}, ...), condition=%wide.region_1.2_spmd, body=%wide.region_0.1_spmd.sunk | while | flops 1208287232 | bytes 17039816 | solution.py:69
  284.8 49.8 %all-gather.15.cloned.1.call-done = f32[4096,128]{1,0:T(8,128)} async-done(((f32[512,128]{1,0:T(8,128)}), f32[4096,128]{1,0:T(8,128)}) %all-gather.15.cloned.1.call-update) | async-done | bytes 2097168 | tf_op jit(solution)/shard_map/while/body/eval_jaxpr/all_gather | solution.py:8
  335.7 3.0 fusion.64
  338.7 2.9 fusion.63
  343.5 49.8 %all-gather.15.cloned.1.call-done = f32[4096,128]{1,0:T(8,128)} async-done(((f32[512,128]{1,0:T(8,128)}), f32[4096,128]{1,0:T(8,128)}) %all-gather.15.cloned.1.call-update) | async-done | bytes 2097168 | tf_op jit(solution)/shard_map/while/body/eval_jaxpr/all_gather | solution.py:8
  394.3 3.0 fusion.64
  397.3 2.9 fusion.63
  402.1 49.8 %all-gather.15.cloned.1.call-done = f32[4096,128]{1,0:T(8,128)} async-done(((f32[512,128]{1,0:T(8,128)}), f32[4096,128]{1,0:T(8,128)}) %all-gather.15.cloned.1.call-update) | async-done | bytes 2097168 | tf_op jit(solution)/shard_map/while/body/eval_jaxpr/all_gather | solution.py:8
  452.9 3.0 fusion.64
  455.9 2.9 fusion.63
  460.7 49.8 %all-gather.15.cloned.1.call-done = f32[4096,128]{1,0:T(8,128)} async-done(((f32[512,128]{1,0:T(8,128)}), f32[4096,128]{1,0:T(8,128)}) %all-gather.15.cloned.1.call-update) | async-done | bytes 2097168 | tf_op jit(solution)/shard_map/while/body/eval_jaxpr/all_gather | solution.py:8
  511.5 3.0 fusion.64
  514.5 2.9 fusion.63
  519.3 49.8 %all-gather.15.cloned.1.call-done = f32[4096,128]{1,0:T(8,128)} async-done(((f32[512,128]{1,0:T(8,128)}), f32[4096,128]{1,0:T(8,128)}) %all-gather.15.cloned.1.call-update) | async-done | bytes 2097168 | tf_op jit(solution)/shard_map/while/body/eval_jaxpr/all_gather | solution.py:8
  570.1 3.0 fusion.64
  573.1 2.9 fusion.63
  577.9 49.8 %all-gather.15.cloned.1.call-done = f32[4096,128]{1,0:T(8,128)} async-done(((f32[512,128]{1,0:T(8,128)}), f32[4096,128]{1,0:T(8,128)}) %all-gather.15.cloned.1.call-update) | async-done | bytes 2097168 | tf_op jit(solution)/shard_map/while/body/eval_jaxpr/all_gather | solution.py:8
  628.7 3.0 fusion.64
  631.8 2.9 fusion.63
  636.5 49.8 %all-gather.15.cloned.1.call-done = f32[4096,128]{1,0:T(8,128)} async-done(((f32[512,128]{1,0:T(8,128)}), f32[4096,128]{1,0:T(8,128)}) %all-gather.15.cloned.1.call-update) | async-done | bytes 2097168 | tf_op jit(solution)/shard_map/while/body/eval_jaxpr/all_gather | solution.py:8
  687.3 3.0 fusion.64
  690.4 2.9 fusion.63
  695.1 49.8 %all-gather.15.cloned.1.call-done = f32[4096,128]{1,0:T(8,128)} async-done(((f32[512,128]{1,0:T(8,128)}), f32[4096,128]{1,0:T(8,128)}) %all-gather.15.cloned.1.call-update) | async-done | bytes 2097168 | tf_op jit(solution)/shard_map/while/body/eval_jaxpr/all_gather | solution.py:8
  745.9 3.0 fusion.64
  748.9 464.0 %while.32 = (s32[]{:T(128)}, f32[2,512,128]{2,1,0:T(8,128)S(1)}, s32[]{:T(128)}, f32[512,8192]{1,0:T(8,128)}, s32[1]{0:T(128)}, /*index=5*/f32[512,8192]{1,0:T(8...) while((s32[]{:T(128)}, f32[2,512,128]{2,1,0:T(8,128)S(1)}, ...), condition=%wide.region_3.4_spmd, body=%wide.region_2.3_spmd.sunk | while | flops 805634048 | bytes 12846105 | solution.py:69
  749.0 2.9 fusion.69
  752.0 51.6 %all-gather.17.cloned.1.call-done = f32[4096,128]{1,0:T(8,128)} async-done(((f32[512,128]{1,0:T(8,128)}), f32[4096,128]{1,0:T(8,128)}) %all-gather.17.cloned.1.call-update) | async-done | bytes 2097168 | tf_op jit(solution)/shard_map/while/body/eval_jaxpr/all_gather | solution.py:8
  807.0 2.9 fusion.69
  810.0 51.6 %all-gather.17.cloned.1.call-done = f32[4096,128]{1,0:T(8,128)} async-done(((f32[512,128]{1,0:T(8,128)}), f32[4096,128]{1,0:T(8,128)}) %all-gather.17.cloned.1.call-update) | async-done | bytes 2097168 | tf_op jit(solution)/shard_map/while/body/eval_jaxpr/all_gather | solution.py:8
  865.0 2.9 fusion.69
  868.0 51.6 %all-gather.17.cloned.1.call-done = f32[4096,128]{1,0:T(8,128)} async-done(((f32[512,128]{1,0:T(8,128)}), f32[4096,128]{1,0:T(8,128)}) %all-gather.17.cloned.1.call-update) | async-done | bytes 2097168 | tf_op jit(solution)/shard_map/while/body/eval_jaxpr/all_gather | solution.py:8
  923.0 2.9 fusion.69
  926.0 51.6 %all-gather.17.cloned.1.call-done = f32[4096,128]{1,0:T(8,128)} async-done(((f32[512,128]{1,0:T(8,128)}), f32[4096,128]{1,0:T(8,128)}) %all-gather.17.cloned.1.call-update) | async-done | bytes 2097168 | tf_op jit(solution)/shard_map/while/body/eval_jaxpr/all_gather | solution.py:8
  981.0 2.9 fusion.69
  984.0 51.6 %all-gather.17.cloned.1.call-done = f32[4096,128]{1,0:T(8,128)} async-done(((f32[512,128]{1,0:T(8,128)}), f32[4096,128]{1,0:T(8,128)}) %all-gather.17.cloned.1.call-update) | async-done | bytes 2097168 | tf_op jit(solution)/shard_map/while/body/eval_jaxpr/all_gather | solution.py:8
  1039.0 2.9 fusion.69
  1042.0 51.6 %all-gather.17.cloned.1.call-done = f32[4096,128]{1,0:T(8,128)} async-done(((f32[512,128]{1,0:T(8,128)}), f32[4096,128]{1,0:T(8,128)}) %all-gather.17.cloned.1.call-update) | async-done | bytes 2097168 | tf_op jit(solution)/shard_map/while/body/eval_jaxpr/all_gather | solution.py:8
  1097.0 2.9 fusion.69
  1100.0 51.6 %all-gather.17.cloned.1.call-done = f32[4096,128]{1,0:T(8,128)} async-done(((f32[512,128]{1,0:T(8,128)}), f32[4096,128]{1,0:T(8,128)}) %all-gather.17.cloned.1.call-update) | async-done | bytes 2097168 | tf_op jit(solution)/shard_map/while/body/eval_jaxpr/all_gather | solution.py:8
  1155.0 2.9 fusion.69
  1158.0 51.6 %all-gather.17.cloned.1.call-done = f32[4096,128]{1,0:T(8,128)} async-done(((f32[512,128]{1,0:T(8,128)}), f32[4096,128]{1,0:T(8,128)}) %all-gather.17.cloned.1.call-update) | async-done | bytes 2097168 | tf_op jit(solution)/shard_map/while/body/eval_jaxpr/all_gather | solution.py:8
  (131 shorter events, 83.2 us)
Async XLA Ops:
  6.5 1.6 copy-start.1
  6.5 179.7 %all-gather.13.cloned.1.call-start = ((), (), s32[]{:S(2)}) async-start(), calls=%async_computation.2 | async-start | bytes 35651584 | tf_op jit(solution)/shard_map/all_gather | solution.py:54
  7.3 272.8 %all-gather.11.cloned.1.call-start = ((), (), s32[]{:S(2)}) async-start(), calls=%async_computation.1 | async-start | bytes 17825792 | tf_op jit(solution)/shard_map/all_gather | solution.py:55
  65.7 1.5 copy-start.2
  71.1 21.1 %all-to-all-start = ((f32[16,1,8192]{2,1,0:T(1,128)}), f32[16,1,8192]{2,1,0:T(1,128)S(1)}, u32[]{:S(2)}, u32[]{:S(2)}) async-start(f32[16,1,8192]{2,1,0:T(1,128)} %reshape.83), calls=%async_computation | async-start | bytes 1048576 | tf_op jit(solution)/shard_map/all_to_all | solution.py:20
  280.1 54.6 %all-gather.15.cloned.1.call-start = ((), (), s32[]{:S(2)}) async-start(), calls=%async_computation.3 | async-start | bytes 2359296 | tf_op jit(solution)/shard_map/while/body/eval_jaxpr/all_gather | solution.py:8
  338.6 54.6 %all-gather.15.cloned.1.call-start = ((), (), s32[]{:S(2)}) async-start(), calls=%async_computation.3 | async-start | bytes 2359296 | tf_op jit(solution)/shard_map/while/body/eval_jaxpr/all_gather | solution.py:8
  397.2 54.6 %all-gather.15.cloned.1.call-start = ((), (), s32[]{:S(2)}) async-start(), calls=%async_computation.3 | async-start | bytes 2359296 | tf_op jit(solution)/shard_map/while/body/eval_jaxpr/all_gather | solution.py:8
  455.8 54.6 %all-gather.15.cloned.1.call-start = ((), (), s32[]{:S(2)}) async-start(), calls=%async_computation.3 | async-start | bytes 2359296 | tf_op jit(solution)/shard_map/while/body/eval_jaxpr/all_gather | solution.py:8
  514.4 54.7 %all-gather.15.cloned.1.call-start = ((), (), s32[]{:S(2)}) async-start(), calls=%async_computation.3 | async-start | bytes 2359296 | tf_op jit(solution)/shard_map/while/body/eval_jaxpr/all_gather | solution.py:8
  573.1 54.6 %all-gather.15.cloned.1.call-start = ((), (), s32[]{:S(2)}) async-start(), calls=%async_computation.3 | async-start | bytes 2359296 | tf_op jit(solution)/shard_map/while/body/eval_jaxpr/all_gather | solution.py:8
  631.7 54.6 %all-gather.15.cloned.1.call-start = ((), (), s32[]{:S(2)}) async-start(), calls=%async_computation.3 | async-start | bytes 2359296 | tf_op jit(solution)/shard_map/while/body/eval_jaxpr/all_gather | solution.py:8
  690.3 54.6 %all-gather.15.cloned.1.call-start = ((), (), s32[]{:S(2)}) async-start(), calls=%async_computation.3 | async-start | bytes 2359296 | tf_op jit(solution)/shard_map/while/body/eval_jaxpr/all_gather | solution.py:8
  748.9 54.6 %all-gather.17.cloned.1.call-start = ((), (), s32[]{:S(2)}) async-start(), calls=%async_computation.4 | async-start | bytes 2359296 | tf_op jit(solution)/shard_map/while/body/eval_jaxpr/all_gather | solution.py:8
  806.9 54.6 %all-gather.17.cloned.1.call-start = ((), (), s32[]{:S(2)}) async-start(), calls=%async_computation.4 | async-start | bytes 2359296 | tf_op jit(solution)/shard_map/while/body/eval_jaxpr/all_gather | solution.py:8
  864.9 54.7 %all-gather.17.cloned.1.call-start = ((), (), s32[]{:S(2)}) async-start(), calls=%async_computation.4 | async-start | bytes 2359296 | tf_op jit(solution)/shard_map/while/body/eval_jaxpr/all_gather | solution.py:8
  922.9 54.6 %all-gather.17.cloned.1.call-start = ((), (), s32[]{:S(2)}) async-start(), calls=%async_computation.4 | async-start | bytes 2359296 | tf_op jit(solution)/shard_map/while/body/eval_jaxpr/all_gather | solution.py:8
  980.9 54.6 %all-gather.17.cloned.1.call-start = ((), (), s32[]{:S(2)}) async-start(), calls=%async_computation.4 | async-start | bytes 2359296 | tf_op jit(solution)/shard_map/while/body/eval_jaxpr/all_gather | solution.py:8
  1038.9 54.6 %all-gather.17.cloned.1.call-start = ((), (), s32[]{:S(2)}) async-start(), calls=%async_computation.4 | async-start | bytes 2359296 | tf_op jit(solution)/shard_map/while/body/eval_jaxpr/all_gather | solution.py:8
  1096.9 54.6 %all-gather.17.cloned.1.call-start = ((), (), s32[]{:S(2)}) async-start(), calls=%async_computation.4 | async-start | bytes 2359296 | tf_op jit(solution)/shard_map/while/body/eval_jaxpr/all_gather | solution.py:8
  1154.9 54.6 %all-gather.17.cloned.1.call-start = ((), (), s32[]{:S(2)}) async-start(), calls=%async_computation.4 | async-start | bytes 2359296 | tf_op jit(solution)/shard_map/while/body/eval_jaxpr/all_gather | solution.py:8
  1212.9 0.8 copy-start
Sparse Core Ops, SparseCore 0:
  9.0 177.1 all-gather.12
  187.9 92.2 all-gather.10
  283.2 51.3 all-gather.14
  341.8 51.4 all-gather.14
  400.4 51.4 all-gather.14
  459.0 51.4 all-gather.14
  517.6 51.4 all-gather.14
  576.2 51.4 all-gather.14
  634.9 51.4 all-gather.14
  693.5 51.4 all-gather.14
  752.1 51.4 all-gather.16
  810.1 51.4 all-gather.16
  868.1 51.4 all-gather.16
  926.1 51.4 all-gather.16
  984.1 51.4 all-gather.16
  1042.1 51.4 all-gather.16
  1100.1 51.4 all-gather.16
  1158.1 51.4 all-gather.16
where the time goes:
time: 1230 us; the launch traced here: 1220 us
  waiting for transfers between devices  999 us (81%)
  matrix products  94.2 us (8%)
  other arithmetic  59.8 us (5%)
  local copies, waits for them, and re-layouts  45.9 us (4%)
  between operations  13.6 us (1%)
    all_gather x16, waiting for transfers between devices, picked(): lax.all_gather(array, axis)  811 us
    all_gather x1, waiting for transfers between devices, on_device(): lax.all_gather(tri_panels, 'col', axis=1, tiled=True)  88.9 us
    all_gather x1, waiting for transfers between devices, on_device(): lax.all_gather(own_inverse, 'col', axis=1, tiled=True)  82.4 us
    dot_general x16, matrix products, advance(): jnp.dot(inverse_block, current, precision=lax.Precision.HIGHEST, preferre...  46.7 us
    dot_general x16, matrix products, advance(): jnp.einsum('sij,jc->sic', pieces, solution, precision=lax.Precision.HIGHEST)  41.8 us
    another operation x4, other arithmetic, on_device(): jax.scipy.linalg.solve_triangular(own_diag, identity_block, lower=True)  41.5 us
  transfers between devices with their start and end apart: 19, of which 19 were waited for; matrix products, arithmetic and copies ran while one was open for 8% of the time, Pallas kernels for 0%

commit v1 on v0

v1 whole, which is shorter than its diff:
```python
import jax
import jax.numpy as jnp
from jax import lax
from jax.sharding import PartitionSpec as P

HI = lax.Precision.HIGHEST


def mm(a, b):
    return jnp.dot(a, b, precision=HI, preferred_element_type=jnp.float32)


def on_device(tri_panels, rhs_rows):
    R = lax.axis_size("row")
    C = lax.axis_size("col")
    p = lax.axis_index("row")
    c = lax.axis_index("col")
    nb = tri_panels.shape[1]
    half = nb // 2
    blocks = tri_panels.shape[0] // nb
    sub = nb // C
    width = rhs_rows.shape[1] // C
    parted = rhs_rows.reshape(blocks, sub, rhs_rows.shape[1])
    state = lax.all_to_all(parted, "col", split_axis=2, concat_axis=1, tiled=True)

    eye = jnp.eye(nb, dtype=jnp.float32)
    own = tri_panels.reshape(blocks, nb, nb)
    is_diag = c % R == p
    diag = lax.dynamic_index_in_dim(own, c // R, 0, keepdims=False)
    diag = jnp.where(is_diag, diag, eye)
    inv = jax.scipy.linalg.solve_triangular(diag, eye, lower=True)
    top = jnp.where(is_diag & (c < R), inv, own[0])
    low = jnp.where(is_diag & (c >= R), inv, own[1])

    moved = lax.ppermute(top[half:], "col", [(i, i + R) for i in range(R)])
    piece = jnp.where(c < R, top[:half], moved)
    g0 = lax.all_gather(piece, "col", axis=0, tiled=False).reshape(2, R, half, nb)
    g1 = lax.all_gather(low, "col", axis=0, tiled=False)

    def block0(k):
        k = jnp.clip(k, 0, R - 1)
        return lax.dynamic_index_in_dim(g0, k, 1, keepdims=False).reshape(nb, nb)

    def block1(k):
        k = jnp.clip(k, 0, C - 1)
        return lax.dynamic_index_in_dim(g1, k, 0, keepdims=False)

    acc0, acc1 = state[0], state[1]
    inv0 = block0(p)
    near0 = mm(inv0, block0(p - 1))
    inv1 = None
    zero = jnp.zeros((nb, width), jnp.float32)
    store = jnp.zeros((R + 1, nb, width), jnp.float32)
    C0 = mm(inv0, acc0)
    mine = jnp.where(p == 0, C0, zero)
    out0 = mine
    C1 = None
    for t in range(C - 1):
        s = t % R
        with jax.named_scope(f"near{t}"):
            P1 = lax.ppermute(mine, "row", [(s, (s + 1) % R)])
        B = [((t - j) % R, (t + 2 + j) % R) for j in range(3) if t - j >= 0 and t + 2 + j < C]
        A = [((t - j) % R, (t + 1 + j) % R) for j in range(1, 4) if t - j >= 0 and t + 1 + j < C]
        XB = XA = None
        with jax.named_scope(f"far{t}"):
            if B:
                XB = lax.ppermute(mine, "row", B)
            if A:
                XA = lax.ppermute(mine, "row", A)
        q = (p - t) % R
        i = t + q
        kA = i - 2 * q + 1
        kB = kA + 1
        inwin = (q >= 2) & (q <= 4)
        if t + 1 < R:
            xc = C0 - mm(near0, P1)
            mine = jnp.where(p == t + 1, xc, mine)
            out0 = mine
            if t > 0:
                pass
            if XB is not None:
                store = lax.dynamic_update_index_in_dim(store, XB, jnp.where(inwin & (kB >= 0), kB, R), 0)
                acc0 = acc0 - mm(block0(kB), XB)
            if XA is not None:
                store = lax.dynamic_update_index_in_dim(store, XA, jnp.where(inwin & (kA >= 0), kA, R), 0)
                acc0 = acc0 - mm(block0(kA), XA)
            store = lax.dynamic_update_index_in_dim(store, P1, jnp.where(p == t + 1, t, R), 0)
            C0 = mm(inv0, acc0)
            if t + 1 == R - 1:
                store = lax.dynamic_update_index_in_dim(store, mine, p, 0)
                inv1 = block1(R + p)
                near1 = mm(inv1, block1(R + p - 1))
                prod = jnp.zeros((nb, width), jnp.float32)
                for k in range(R):
                    prod = prod + mm(g1[k], store[k])
                acc1 = acc1 - prod
                C1 = mm(inv1, acc1)
        else:
            xc = C1 - mm(near1, P1)
            mine = jnp.where(p == (t + 1) - R, xc, mine)
            if XB is not None:
                acc1 = acc1 - mm(block1(kB), XB)
            if XA is not None:
                acc1 = acc1 - mm(block1(kA), XA)
            C1 = mm(inv1, acc1)
    return jnp.concatenate([out0, mine], 0)


def solution(mesh):
    return jax.shard_map(
        on_device,
        mesh=mesh,
        in_specs=(P("row", "col"), P(("row", "col"), None)),
        out_specs=P("row", "col"),
        check_vma=False,
    )
```

time: 1230 us -> 402 us (0.33)
  waiting for transfers between devices: 999 us -> 155 us
  starting transfers between devices: 6.47 us -> 64.3 us
  local copies, waits for them, and re-layouts: 45.9 us -> 26.5 us
  other arithmetic: 59.8 us -> 46.1 us
    all_gather x18 -> x2, waiting for transfers between devices: 983 us -> 26.9 us  [the longest x1 26.9 us: on_device(): lax.all_gather(piece, 'col', axis=0, tiled=False).reshape(2, R, half, nb)]
    ppermute x0 -> x43, waiting for transfers between devices: none -> 113 us  [the longest x14 90.6 us: on_device(): XB = lax.ppermute(mine, 'row', B)]
    ppermute x0 -> x43, starting transfers between devices: none -> 56.9 us  [the longest x14 21.2 us: on_device(): XB = lax.ppermute(mine, 'row', B)]
    dynamic_update_slice x16 -> x0, other arithmetic: 15.8 us -> none  [advance(): lax.dynamic_update_index_in_dim(state_rhs, stored, slot_index, 0)]
    dot_general x32 -> x65, matrix products: 88.5 us -> 79.1 us  [mm(): return jnp.dot(a, b, precision=HI, preferred_element_type=jnp.float32)]
    another operation x4 -> x3, other arithmetic: 41.5 us -> 41 us  [on_device(): inv = jax.scipy.linalg.solve_triangular(diag, eye, lower=True)]
  transfers between devices with their start and end apart: 19 -> 46, of which waited for: 19 -> 12; matrix products, arithmetic and copies ran while one was open for 8% -> 25% of each run, Pallas kernels for 0% -> 0%
where the time goes in v1:
time: 402 us; the launch traced here: 395 us
  waiting for transfers between devices  155 us (39%)
  matrix products  86.8 us (22%)
  starting transfers between devices  64.3 us (16%)
  other arithmetic  46.1 us (11%)
  local copies, waits for them, and re-layouts  26.5 us (7%)
  between operations  16 us (4%)
    ppermute x14, waiting for transfers between devices, on_device(): XB = lax.ppermute(mine, 'row', B)  90.6 us
    dot_general x65, matrix products, mm(): return jnp.dot(a, b, precision=HI, preferred_element_type=jnp.float32)  79.1 us
    another operation x3, other arithmetic, on_device(): inv = jax.scipy.linalg.solve_triangular(diag, eye, lower=True)  41 us
    all_gather x1, waiting for transfers between devices, on_device(): lax.all_gather(piece, 'col', axis=0, tiled=False).reshape(2, R, half, nb)  26.9 us
    ppermute x14, starting transfers between devices, on_device(): XB = lax.ppermute(mine, 'row', B)  21.2 us
    ppermute x13, starting transfers between devices, on_device(): XA = lax.ppermute(mine, 'row', A)  16.6 us
    all_to_all x1, waiting for transfers between devices, on_device(): lax.all_to_all(parted, 'col', split_axis=2, concat_axis=1, tiled=True)  14.3 us
    ppermute x15, starting transfers between devices, on_device(): P1 = lax.ppermute(mine, 'row', [(s, (s + 1) % R)])  13.9 us
  transfers between devices with their start and end apart: 46, of which 12 were waited for; matrix products, arithmetic and copies ran while one was open for 25% of the time, Pallas kernels for 0%

profile of v1, /device:TPU:120, one launch (start us, length us, event | category | flops | bytes accessed | tf_op | source)
XLA Modules:
  0.0 394.6 jit_solution(1622500313571051565)
XLA Ops:
  6.8 1.7 fusion.77
  8.5 8.0 %while.1 = (s32[]{:T(128)}, f32[512,512]{1,0:T(8,128)S(1)}, s32[4,2]{0,1:T(2,128)S(1)}, f32[4,128,128]{2,1,0:T(8,128)S(1)}, s32[]{:T(128)}) while((s32[]{:T(128)}, f32[512,512]{1,0:T(8,128)S(1)}, s32[4,2]{0,1:T(2,128)S(1)}, f32[4,128,128]{2,1,0:T(8,128)S(1)}, s32[]{:T(128)}) %tuple.35), condition=%wide.while_cond, body=%wide.while_body.sunk | while | flops 2 | bytes 131181 | solution.py:31
  9.2 1.3 bitcast_dynamic-update-slice_fusion.23
  11.2 1.3 bitcast_dynamic-update-slice_fusion.23
  13.2 1.3 bitcast_dynamic-update-slice_fusion.23
  15.2 1.3 bitcast_dynamic-update-slice_fusion.23
  16.5 39.3 %custom-call.4 = f32[4,128,128]{1,2,0:T(8,128)S(1)} custom-call(f32[4,128,128]{2,1,0:T(8,128)S(1)} %get-tuple-element.12), custom_call_target="InvertDiagBlocksLowerTriangular" | custom-call | tf_op jit(solution)/shard_map/jit(_solve_triangular)/triangular_solve | solution.py:31
  56.9 1.4 fusion.118
  58.4 1.4 convolution_subtract_fusion
  61.1 1.7 convolution_subtract_fusion.2
  65.4 5.1 %collective-permute-start = (f32[256,512]{1,0:T(8,128)S(1)}, f32[256,512]{1,0:T(8,128)S(1)}, u32[]{:S(2)}, u32[]{:S(2)}) collective-permute-start(f32[256,512]{1,0:T(8,128)S(1)} %slice.145), channel_id=1, source_target_pairs={{0,8},{1,9},{2,10},{3,11},{4,12},{5,13},{6,14},{7,15},{16,24},{17,... | collective-permute-start | bytes 1572872 | tf_op jit(solution)/shard_map/ppermute | solution.py:35
  70.5 11.1 %collective-permute-done = f32[256,512]{1,0:T(8,128)S(1)} collective-permute-done((f32[256,512]{1,0:T(8,128)S(1)}, f32[256,512]{1,0:T(8,128)S(1)}, u32[]{:S(2)}, u32[]{:S(2)}) %collective-permute-start) | collective-permute-done | bytes 524320 | tf_op jit(solution)/shard_map/ppermute | solution.py:35
  84.3 2.8 reshape.149
  87.2 7.3 %all-to-all-start = ((f32[16,1,8192]{2,1,0:T(1,128)}), f32[16,1,8192]{2,1,0:T(1,128)S(1)}, u32[]{:S(2)}, u32[]{:S(2)}) async-start(f32[16,1,8192]{2,1,0:T(1,128)} %reshape.149), calls=%async_computation | async-start | bytes 1048576 | tf_op jit(solution)/shard_map/all_to_all | solution.py:24
  95.2 14.3 %all-to-all-done = f32[16,1,8192]{2,1,0:T(1,128)S(1)} async-done(((f32[16,1,8192]{2,1,0:T(1,128)}), f32[16,1,8192]{2,1,0:T(1,128)S(1)}, u32[]{:S(2)}, u32[]{:S(2)}) %all-to-all-start) | async-done | bytes 524320 | tf_op jit(solution)/shard_map/all_to_all | solution.py:24
  110.0 1.9 reduce
  111.8 1.8 reshape.150
  115.4 26.9 %all-gather.5.cloned.1.call-done = f32[4096,512]{1,0:T(8,128)} async-done(((f32[256,512]{1,0:T(8,128)}), f32[4096,512]{1,0:T(8,128)}) %all-gather.5.cloned.1.call-update) | async-done | bytes 8388624 | tf_op jit(solution)/shard_map/all_gather | solution.py:37
  142.3 9.5 %constant_dynamic-slice_fusion.2 = (f32[2,1,256,512]{3,2,1,0:T(8,128)}, f32[2,1,256,512]{3,2,1,0:T(8,128)}, f32[2,1,256,512]{3,2,1,0:T(8,128)}, f32[2,1,256,512]...) fusion(f32[2,8,256,512]{3,2,1,0:T(8,128)} %bitcast.304, ...), kind=kLoop, calls=%fused_computation.225 | loop fusion | bytes 27263028 | tf_op jit(solution)/shard_map/jit(dynamic_index_in_dim)/dynamic_slice | solution.py:42
  154.2 1.8 fusion.146
  179.7 28.3 %collective-permute-done.9 = f32[512,128]{1,0:T(8,128)S(1)} collective-permute-done((f32[512,128]{1,0:T(8,128)S(1)}, f32[512,128]{1,0:T(8,128)S(1)}, u32[]{:S(2)}, u32[]{:S(2)}) %collective-permute-start.9) | collective-permute-done | bytes 262176 | tf_op jit(solution)/shard_map/far3/ppermute | solution.py:67
  215.8 23.7 %collective-permute-done.12 = f32[512,128]{1,0:T(8,128)S(1)} collective-permute-done((f32[512,128]{1,0:T(8,128)S(1)}, f32[512,128]{1,0:T(8,128)S(1)}, u32[]{:S(2)}, u32[]{:S(2)}) %collective-permute-start.12) | collective-permute-done | bytes 262176 | tf_op jit(solution)/shard_map/far4/ppermute | solution.py:67
  246.3 10.9 %collective-permute-done.15 = f32[512,128]{1,0:T(8,128)S(1)} collective-permute-done((f32[512,128]{1,0:T(8,128)S(1)}, f32[512,128]{1,0:T(8,128)S(1)}, u32[]{:S(2)}, u32[]{:S(2)}) %collective-permute-start.15) | collective-permute-done | bytes 262176 | tf_op jit(solution)/shard_map/far5/ppermute | solution.py:67
  261.5 1.4 collective-permute-start.22
  262.9 6.9 %collective-permute-start.21 = (f32[512,128]{1,0:T(8,128)S(1)}, f32[512,128]{1,0:T(8,128)S(1)}, u32[]{:S(2)}, u32[]{:S(2)}) collective-permute-start(f32[512,128]{1,0:T(8,128)S(1)} %get-tuple-element.43), channel_id=1, source_target_pairs={{112,16},{96,32},{80,48},{113,17},{97,33},{81,49},{114,18},{98,34}... | collective-permute-start | bytes 786440 | tf_op jit(solution)/shard_map/far7/ppermute | solution.py:67
  269.8 2.0 collective-permute-start.23
  271.9 2.4 fusion.35
  274.3 2.8 convolution_add_fusion.6
  277.1 2.4 convolution_add_fusion.5
  279.5 2.2 convolution_add_fusion.4
  281.7 2.2 convolution_add_fusion.3
  283.9 2.2 convolution_add_fusion.2
  286.1 2.2 convolution_add_fusion.1
  288.4 2.2 fusion.15
  290.6 3.4 fusion.54
  296.9 1.3 collective-permute-start.25
  298.2 1.3 collective-permute-start.24
  299.5 1.9 fusion.57
  304.5 1.3 collective-permute-start.28
  308.8 8.4 %collective-permute-done.24 = f32[512,128]{1,0:T(8,128)S(1)} collective-permute-done((f32[512,128]{1,0:T(8,128)S(1)}, f32[512,128]{1,0:T(8,128)S(1)}, u32[]{:S(2)}, u32[]{:S(2)}) %collective-permute-start.24) | collective-permute-done | bytes 262176 | tf_op jit(solution)/shard_map/far8/ppermute | solution.py:67
  320.9 2.8 collective-permute-start.31
  338.1 1.5 collective-permute-start.36
  339.6 2.8 collective-permute-done.34
  343.4 15.8 %collective-permute-done.33 = f32[512,128]{1,0:T(8,128)S(1)} collective-permute-done((f32[512,128]{1,0:T(8,128)S(1)}, f32[512,128]{1,0:T(8,128)S(1)}, u32[]{:S(2)}, u32[]{:S(2)}) %collective-permute-start.33) | collective-permute-done | bytes 262176 | tf_op jit(solution)/shard_map/far11/ppermute | solution.py:67
  369.4 1.5 collective-permute-start.42
  370.9 3.8 collective-permute-done.40
  375.8 3.4 collective-permute-done.39
  381.2 4.6 %collective-permute-done.42 = f32[512,128]{1,0:T(8,128)S(1)} collective-permute-done((f32[512,128]{1,0:T(8,128)S(1)}, f32[512,128]{1,0:T(8,128)S(1)}, u32[]{:S(2)}, u32[]{:S(2)}) %collective-permute-start.42) | collective-permute-done | bytes 262176 | tf_op jit(solution)/shard_map/near14/ppermute | solution.py:61
  (213 shorter events, 99.4 us)
Async XLA Ops:
  6.5 135.8 %all-gather.5.cloned.1.call-start = ((), (), s32[]{:S(2)}) async-start(), calls=%async_computation.1 | async-start | bytes 8912896 | tf_op jit(solution)/shard_map/all_gather | solution.py:37
  6.7 49.4 %copy-start.13 = (f32[512,512]{1,0:T(8,128)}, f32[512,512]{1,0:T(8,128)S(1)}, u32[]{:S(2)}) copy-start(f32[512,512]{1,0:T(8,128)S(1)} %fusion.110) | copy-start | bytes 3145732
  16.5 39.7 %copy-start.14 = (f32[512,512]{1,0:T(8,128)}, f32[512,512]{1,0:T(8,128)S(1)}, u32[]{:S(2)}) copy-start(f32[512,512]{1,0:T(8,128)S(1)} %get-tuple-element.94) | copy-start | bytes 3145732
  65.4 16.2 %collective-permute-start = (f32[256,512]{1,0:T(8,128)S(1)}, f32[256,512]{1,0:T(8,128)S(1)}, u32[]{:S(2)}, u32[]{:S(2)}) collective-permute-start(f32[256,512]{1,0:T(8,128)S(1)} %slice.145), channel_id=1, source_target_pairs={{0,8},{1,9},{2,10},{3,11},{4,12},{5,13},{6,14},{7,15},{16,24},{17,... | collective-permute-start | bytes 1572872 | tf_op jit(solution)/shard_map/ppermute | solution.py:35
  82.5 189.3 %all-gather.7.cloned.1.call-start = ((), (), s32[]{:S(2)}) async-start(), calls=%async_computation.2 | async-start | bytes 17825792 | tf_op jit(solution)/shard_map/all_gather | solution.py:38
  87.2 22.3 %all-to-all-start = ((f32[16,1,8192]{2,1,0:T(1,128)}), f32[16,1,8192]{2,1,0:T(1,128)S(1)}, u32[]{:S(2)}, u32[]{:S(2)}) async-start(f32[16,1,8192]{2,1,0:T(1,128)} %reshape.149), calls=%async_computation | async-start | bytes 1048576 | tf_op jit(solution)/shard_map/all_to_all | solution.py:24
  152.8 3.2 collective-permute-start.2
  153.5 5.8 %collective-permute-start.1 = (f32[512,128]{1,0:T(8,128)S(1)}, f32[512,128]{1,0:T(8,128)S(1)}, u32[]{:S(2)}, u32[]{:S(2)}) collective-permute-start(f32[512,128]{1,0:T(8,128)S(1)} %get-tuple-element.40), channel_id=1, source_target_pairs={{0,32},{1,33},{2,34},{3,35},{4,36},{5,37},{6,38},{7,39},{8,40},{9,... | collective-permute-start | bytes 786440 | tf_op jit(solution)/shard_map/far0/ppermute | solution.py:67
  157.1 7.6 %collective-permute-start.4 = (f32[512,128]{1,0:T(8,128)S(1)}, f32[512,128]{1,0:T(8,128)S(1)}, u32[]{:S(2)}, u32[]{:S(2)}) collective-permute-start(f32[512,128]{1,0:T(8,128)S(1)} %fusion.27), channel_id=1, source_target_pairs={{0,48},{1,49},{2,50},{3,51},{4,52},{5,53},{6,54},{7,55},{8,56},{9,... | collective-permute-start | bytes 786440 | tf_op jit(solution)/shard_map/far1/ppermute | solution.py:69
  157.7 6.9 %collective-permute-start.3 = (f32[512,128]{1,0:T(8,128)S(1)}, f32[512,128]{1,0:T(8,128)S(1)}, u32[]{:S(2)}, u32[]{:S(2)}) collective-permute-start(f32[512,128]{1,0:T(8,128)S(1)} %fusion.27), channel_id=1, source_target_pairs={{16,48},{0,64},{17,49},{1,65},{18,50},{2,66},{19,51},{3,67},{20,52... | collective-permute-start | bytes 786440 | tf_op jit(solution)/shard_map/far1/ppermute | solution.py:67
  158.4 3.2 collective-permute-start.5
  162.6 5.2 %collective-permute-start.8 = (f32[512,128]{1,0:T(8,128)S(1)}, f32[512,128]{1,0:T(8,128)S(1)}, u32[]{:S(2)}, u32[]{:S(2)}) collective-permute-start(f32[512,128]{1,0:T(8,128)S(1)} %fusion.25), channel_id=1, source_target_pairs={{32,48},{33,49},{34,50},{35,51},{36,52},{37,53},{38,54},{39,55},{4... | collective-permute-start | bytes 786440 | tf_op jit(solution)/shard_map/near2/ppermute | solution.py:61
  163.3 9.1 %collective-permute-start.7 = (f32[512,128]{1,0:T(8,128)S(1)}, f32[512,128]{1,0:T(8,128)S(1)}, u32[]{:S(2)}, u32[]{:S(2)}) collective-permute-start(f32[512,128]{1,0:T(8,128)S(1)} %fusion.25), channel_id=1, source_target_pairs={{16,64},{0,80},{17,65},{1,81},{18,66},{2,82},{19,67},{3,83},{20,68... | collective-permute-start | bytes 786440 | tf_op jit(solution)/shard_map/far2/ppermute | solution.py:69
  164.0 8.3 %collective-permute-start.6 = (f32[512,128]{1,0:T(8,128)S(1)}, f32[512,128]{1,0:T(8,128)S(1)}, u32[]{:S(2)}, u32[]{:S(2)}) collective-permute-start(f32[512,128]{1,0:T(8,128)S(1)} %fusion.25), channel_id=1, source_target_pairs={{32,64},{16,80},{0,96},{33,65},{17,81},{1,97},{34,66},{18,82},{2,9... | collective-permute-start | bytes 786440 | tf_op jit(solution)/shard_map/far2/ppermute | solution.py:67
  168.8 39.3 %collective-permute-start.10 = (f32[512,128]{1,0:T(8,128)S(1)}, f32[512,128]{1,0:T(8,128)S(1)}, u32[]{:S(2)}, u32[]{:S(2)}) collective-permute-start(f32[512,128]{1,0:T(8,128)S(1)} %fusion.23), channel_id=1, source_target_pairs={{32,80},{16,96},{0,112},{33,81},{17,97},{1,113},{34,82},{18,98},{2... | collective-permute-start | bytes 786440 | tf_op jit(solution)/shard_map/far3/ppermute | solution.py:69
  170.1 37.9 %collective-permute-start.9 = (f32[512,128]{1,0:T(8,128)S(1)}, f32[512,128]{1,0:T(8,128)S(1)}, u32[]{:S(2)}, u32[]{:S(2)}) collective-permute-start(f32[512,128]{1,0:T(8,128)S(1)} %fusion.23), channel_id=1, source_target_pairs={{48,80},{32,96},{16,112},{49,81},{33,97},{17,113},{50,82},{34,98},... | collective-permute-start | bytes 786440 | tf_op jit(solution)/shard_map/far3/ppermute | solution.py:67
  171.4 4.0 %collective-permute-start.11 = (f32[512,128]{1,0:T(8,128)S(1)}, f32[512,128]{1,0:T(8,128)S(1)}, u32[]{:S(2)}, u32[]{:S(2)}) collective-permute-start(f32[512,128]{1,0:T(8,128)S(1)} %fusion.23), channel_id=1, source_target_pairs={{48,64},{49,65},{50,66},{51,67},{52,68},{53,69},{54,70},{55,71},{5... | collective-permute-start | bytes 786440 | tf_op jit(solution)/shard_map/near3/ppermute | solution.py:61
  176.4 34.7 %collective-permute-start.14 = (f32[512,128]{1,0:T(8,128)S(1)}, f32[512,128]{1,0:T(8,128)S(1)}, u32[]{:S(2)}, u32[]{:S(2)}) collective-permute-start(f32[512,128]{1,0:T(8,128)S(1)} %fusion.21), channel_id=1, source_target_pairs={{64,80},{65,81},{66,82},{67,83},{68,84},{69,85},{70,86},{71,87},{7... | collective-permute-start | bytes 786440 | tf_op jit(solution)/shard_map/near4/ppermute | solution.py:61
  177.1 62.5 %collective-permute-start.13 = (f32[512,128]{1,0:T(8,128)S(1)}, f32[512,128]{1,0:T(8,128)S(1)}, u32[]{:S(2)}, u32[]{:S(2)}) collective-permute-start(f32[512,128]{1,0:T(8,128)S(1)} %fusion.21), channel_id=1, source_target_pairs={{48,96},{32,112},{16,0},{49,97},{33,113},{17,1},{50,98},{34,114},{... | collective-permute-start | bytes 786440 | tf_op jit(solution)/shard_map/far4/ppermute | solution.py:69
  178.4 61.1 %collective-permute-start.12 = (f32[512,128]{1,0:T(8,128)S(1)}, f32[512,128]{1,0:T(8,128)S(1)}, u32[]{:S(2)}, u32[]{:S(2)}) collective-permute-start(f32[512,128]{1,0:T(8,128)S(1)} %fusion.21), channel_id=1, source_target_pairs={{64,96},{48,112},{32,0},{65,97},{49,113},{33,1},{66,98},{50,114},{... | collective-permute-start | bytes 786440 | tf_op jit(solution)/shard_map/far4/ppermute | solution.py:67
  212.2 45.2 %collective-permute-start.16 = (f32[512,128]{1,0:T(8,128)S(1)}, f32[512,128]{1,0:T(8,128)S(1)}, u32[]{:S(2)}, u32[]{:S(2)}) collective-permute-start(f32[512,128]{1,0:T(8,128)S(1)} %fusion.19), channel_id=1, source_target_pairs={{64,112},{48,0},{32,16},{65,113},{49,1},{33,17},{66,114},{50,2},{3... | collective-permute-start | bytes 786440 | tf_op jit(solution)/shard_map/far5/ppermute | solution.py:69
  213.5 43.8 %collective-permute-start.15 = (f32[512,128]{1,0:T(8,128)S(1)}, f32[512,128]{1,0:T(8,128)S(1)}, u32[]{:S(2)}, u32[]{:S(2)}) collective-permute-start(f32[512,128]{1,0:T(8,128)S(1)} %fusion.19), channel_id=1, source_target_pairs={{80,112},{64,0},{48,16},{81,113},{65,1},{49,17},{82,114},{66,2},{5... | collective-permute-start | bytes 786440 | tf_op jit(solution)/shard_map/far5/ppermute | solution.py:67
  214.8 27.9 %collective-permute-start.17 = (f32[512,128]{1,0:T(8,128)S(1)}, f32[512,128]{1,0:T(8,128)S(1)}, u32[]{:S(2)}, u32[]{:S(2)}) collective-permute-start(f32[512,128]{1,0:T(8,128)S(1)} %fusion.19), channel_id=1, source_target_pairs={{80,96},{81,97},{82,98},{83,99},{84,100},{85,101},{86,102},{87,103... | collective-permute-start | bytes 786440 | tf_op jit(solution)/shard_map/near5/ppermute | solution.py:61
  243.7 16.7 %collective-permute-start.19 = (f32[512,128]{1,0:T(8,128)S(1)}, f32[512,128]{1,0:T(8,128)S(1)}, u32[]{:S(2)}, u32[]{:S(2)}) collective-permute-start(f32[512,128]{1,0:T(8,128)S(1)} %fusion.17), channel_id=1, source_target_pairs={{96,0},{80,16},{64,32},{97,1},{81,17},{65,33},{98,2},{82,18},{66,3... | collective-permute-start | bytes 786440 | tf_op jit(solution)/shard_map/far6/ppermute | solution.py:67
  244.4 16.1 %collective-permute-start.20 = (f32[512,128]{1,0:T(8,128)S(1)}, f32[512,128]{1,0:T(8,128)S(1)}, u32[]{:S(2)}, u32[]{:S(2)}) collective-permute-start(f32[512,128]{1,0:T(8,128)S(1)} %fusion.17), channel_id=1, source_target_pairs={{80,0},{64,16},{48,32},{81,1},{65,17},{49,33},{82,2},{66,18},{50,3... | collective-permute-start | bytes 786440 | tf_op jit(solution)/shard_map/far6/ppermute | solution.py:69
  245.0 15.4 %collective-permute-start.18 = (f32[512,128]{1,0:T(8,128)S(1)}, f32[512,128]{1,0:T(8,128)S(1)}, u32[]{:S(2)}, u32[]{:S(2)}) collective-permute-start(f32[512,128]{1,0:T(8,128)S(1)} %fusion.17), channel_id=1, source_target_pairs={{96,112},{97,113},{98,114},{99,115},{100,116},{101,117},{102,118},... | collective-permute-start | bytes 786440 | tf_op jit(solution)/shard_map/near6/ppermute | solution.py:61
  261.5 38.0 %collective-permute-start.22 = (f32[512,128]{1,0:T(8,128)S(1)}, f32[512,128]{1,0:T(8,128)}, u32[]{:S(2)}, u32[]{:S(2)}) collective-permute-start(f32[512,128]{1,0:T(8,128)S(1)} %get-tuple-element.43), channel_id=1, source_target_pairs={{96,16},{80,32},{64,48},{97,17},{81,33},{65,49},{98,18},{82,34},{6... | collective-permute-start | bytes 786440 | tf_op jit(solution)/shard_map/far7/ppermute | solution.py:69
  262.9 38.6 %collective-permute-start.21 = (f32[512,128]{1,0:T(8,128)S(1)}, f32[512,128]{1,0:T(8,128)S(1)}, u32[]{:S(2)}, u32[]{:S(2)}) collective-permute-start(f32[512,128]{1,0:T(8,128)S(1)} %get-tuple-element.43), channel_id=1, source_target_pairs={{112,16},{96,32},{80,48},{113,17},{97,33},{81,49},{114,18},{98,34}... | collective-permute-start | bytes 786440 | tf_op jit(solution)/shard_map/far7/ppermute | solution.py:67
  269.8 25.2 %collective-permute-start.23 = (f32[512,128]{1,0:T(8,128)S(1)}, f32[512,128]{1,0:T(8,128)S(1)}, u32[]{:S(2)}, u32[]{:S(2)}) collective-permute-start(f32[512,128]{1,0:T(8,128)S(1)} %get-tuple-element.43), channel_id=1, source_target_pairs={{112,0},{113,1},{114,2},{115,3},{116,4},{117,5},{118,6},{119,7},{1... | collective-permute-start | bytes 786440 | tf_op jit(solution)/shard_map/near7/ppermute | solution.py:61
  296.0 7.5 %collective-permute-start.26 = (f32[512,128]{1,0:T(8,128)S(1)}, f32[512,128]{1,0:T(8,128)S(1)}, u32[]{:S(2)}, u32[]{:S(2)}) collective-permute-start(f32[512,128]{1,0:T(8,128)S(1)} %fusion.13), channel_id=1, source_target_pairs={{0,16},{1,17},{2,18},{3,19},{4,20},{5,21},{6,22},{7,23},{8,24},{9,... | collective-permute-start | bytes 786440 | tf_op jit(solution)/shard_map/near8/ppermute | solution.py:61
  296.9 10.9 %collective-permute-start.25 = (f32[512,128]{1,0:T(8,128)S(1)}, f32[512,128]{1,0:T(8,128)S(1)}, u32[]{:S(2)}, u32[]{:S(2)}) collective-permute-start(f32[512,128]{1,0:T(8,128)S(1)} %fusion.13), channel_id=1, source_target_pairs={{112,32},{96,48},{80,64},{113,33},{97,49},{81,65},{114,34},{98,50}... | collective-permute-start | bytes 786440 | tf_op jit(solution)/shard_map/far8/ppermute | solution.py:69
  298.2 19.0 %collective-permute-start.24 = (f32[512,128]{1,0:T(8,128)S(1)}, f32[512,128]{1,0:T(8,128)S(1)}, u32[]{:S(2)}, u32[]{:S(2)}) collective-permute-start(f32[512,128]{1,0:T(8,128)S(1)} %fusion.13), channel_id=1, source_target_pairs={{0,32},{112,48},{96,64},{1,33},{113,49},{97,65},{2,34},{114,50},{9... | collective-permute-start | bytes 786440 | tf_op jit(solution)/shard_map/far8/ppermute | solution.py:67
  304.5 20.4 %collective-permute-start.28 = (f32[512,128]{1,0:T(8,128)S(1)}, f32[512,128]{1,0:T(8,128)S(1)}, u32[]{:S(2)}, u32[]{:S(2)}) collective-permute-start(f32[512,128]{1,0:T(8,128)S(1)} %fusion.11), channel_id=1, source_target_pairs={{0,48},{112,64},{96,80},{1,49},{113,65},{97,81},{2,50},{114,66},{9... | collective-permute-start | bytes 786440 | tf_op jit(solution)/shard_map/far9/ppermute | solution.py:69
  305.8 20.0 %collective-permute-start.27 = (f32[512,128]{1,0:T(8,128)S(1)}, f32[512,128]{1,0:T(8,128)S(1)}, u32[]{:S(2)}, u32[]{:S(2)}) collective-permute-start(f32[512,128]{1,0:T(8,128)S(1)} %fusion.11), channel_id=1, source_target_pairs={{16,48},{0,64},{112,80},{17,49},{1,65},{113,81},{18,50},{2,66},{11... | collective-permute-start | bytes 786440 | tf_op jit(solution)/shard_map/far9/ppermute | solution.py:67
  307.1 12.1 %collective-permute-start.29 = (f32[512,128]{1,0:T(8,128)S(1)}, f32[512,128]{1,0:T(8,128)S(1)}, u32[]{:S(2)}, u32[]{:S(2)}) collective-permute-start(f32[512,128]{1,0:T(8,128)S(1)} %fusion.11), channel_id=1, source_target_pairs={{16,32},{17,33},{18,34},{19,35},{20,36},{21,37},{22,38},{23,39},{2... | collective-permute-start | bytes 786440 | tf_op jit(solution)/shard_map/near9/ppermute | solution.py:61
  320.2 7.6 %collective-permute-start.32 = (f32[512,128]{1,0:T(8,128)S(1)}, f32[512,128]{1,0:T(8,128)S(1)}, u32[]{:S(2)}, u32[]{:S(2)}) collective-permute-start(f32[512,128]{1,0:T(8,128)S(1)} %fusion.9), channel_id=1, source_target_pairs={{32,48},{33,49},{34,50},{35,51},{36,52},{37,53},{38,54},{39,55},{4... | collective-permute-start | bytes 786440 | tf_op jit(solution)/shard_map/near10/ppermute | solution.py:61
  320.9 11.2 %collective-permute-start.31 = (f32[512,128]{1,0:T(8,128)S(1)}, f32[512,128]{1,0:T(8,128)S(1)}, u32[]{:S(2)}, u32[]{:S(2)}) collective-permute-start(f32[512,128]{1,0:T(8,128)S(1)} %fusion.9), channel_id=1, source_target_pairs={{16,64},{0,80},{112,96},{17,65},{1,81},{113,97},{18,66},{2,82},{11... | collective-permute-start | bytes 786440 | tf_op jit(solution)/shard_map/far10/ppermute | solution.py:69
  323.7 9.4 %collective-permute-start.30 = (f32[512,128]{1,0:T(8,128)S(1)}, f32[512,128]{1,0:T(8,128)S(1)}, u32[]{:S(2)}, u32[]{:S(2)}) collective-permute-start(f32[512,128]{1,0:T(8,128)S(1)} %fusion.9), channel_id=1, source_target_pairs={{32,64},{16,80},{0,96},{33,65},{17,81},{1,97},{34,66},{18,82},{2,9... | collective-permute-start | bytes 786440 | tf_op jit(solution)/shard_map/far10/ppermute | solution.py:67
  328.8 13.6 %collective-permute-start.34 = (f32[512,128]{1,0:T(8,128)S(1)}, f32[512,128]{1,0:T(8,128)S(1)}, u32[]{:S(2)}, u32[]{:S(2)}) collective-permute-start(f32[512,128]{1,0:T(8,128)S(1)} %fusion.7), channel_id=1, source_target_pairs={{32,80},{16,96},{0,112},{33,81},{17,97},{1,113},{34,82},{18,98},{2... | collective-permute-start | bytes 786440 | tf_op jit(solution)/shard_map/far11/ppermute | solution.py:69
  330.1 29.0 %collective-permute-start.33 = (f32[512,128]{1,0:T(8,128)S(1)}, f32[512,128]{1,0:T(8,128)S(1)}, u32[]{:S(2)}, u32[]{:S(2)}) collective-permute-start(f32[512,128]{1,0:T(8,128)S(1)} %fusion.7), channel_id=1, source_target_pairs={{48,80},{32,96},{16,112},{49,81},{33,97},{17,113},{50,82},{34,98},... | collective-permute-start | bytes 786440 | tf_op jit(solution)/shard_map/far11/ppermute | solution.py:67
  331.4 3.7 collective-permute-start.35
  336.1 25.0 %collective-permute-start.38 = (f32[512,128]{1,0:T(8,128)S(1)}, f32[512,128]{1,0:T(8,128)S(1)}, u32[]{:S(2)}, u32[]{:S(2)}) collective-permute-start(f32[512,128]{1,0:T(8,128)S(1)} %fusion.5), channel_id=1, source_target_pairs={{64,80},{65,81},{66,82},{67,83},{68,84},{69,85},{70,86},{71,87},{7... | collective-permute-start | bytes 786440 | tf_op jit(solution)/shard_map/near12/ppermute | solution.py:61
  336.8 28.6 %collective-permute-start.37 = (f32[512,128]{1,0:T(8,128)S(1)}, f32[512,128]{1,0:T(8,128)S(1)}, u32[]{:S(2)}, u32[]{:S(2)}) collective-permute-start(f32[512,128]{1,0:T(8,128)S(1)} %fusion.5), channel_id=1, source_target_pairs={{48,96},{32,112},{49,97},{33,113},{50,98},{34,114},{51,99},{35,115... | collective-permute-start | bytes 786440 | tf_op jit(solution)/shard_map/far12/ppermute | solution.py:69
  338.1 28.3 %collective-permute-start.36 = (f32[512,128]{1,0:T(8,128)S(1)}, f32[512,128]{1,0:T(8,128)S(1)}, u32[]{:S(2)}, u32[]{:S(2)}) collective-permute-start(f32[512,128]{1,0:T(8,128)S(1)} %fusion.5), channel_id=1, source_target_pairs={{64,96},{48,112},{65,97},{49,113},{66,98},{50,114},{67,99},{51,115... | collective-permute-start | bytes 786440 | tf_op jit(solution)/shard_map/far12/ppermute | solution.py:67
  362.1 12.6 %collective-permute-start.40 = (f32[512,128]{1,0:T(8,128)S(1)}, f32[512,128]{1,0:T(8,128)S(1)}, u32[]{:S(2)}, u32[]{:S(2)}) collective-permute-start(f32[512,128]{1,0:T(8,128)S(1)} %fusion.3), channel_id=1, source_target_pairs={{64,112},{65,113},{66,114},{67,115},{68,116},{69,117},{70,118},{71... | collective-permute-start | bytes 786440 | tf_op jit(solution)/shard_map/far13/ppermute | solution.py:69
  363.4 15.7 %collective-permute-start.39 = (f32[512,128]{1,0:T(8,128)S(1)}, f32[512,128]{1,0:T(8,128)S(1)}, u32[]{:S(2)}, u32[]{:S(2)}) collective-permute-start(f32[512,128]{1,0:T(8,128)S(1)} %fusion.3), channel_id=1, source_target_pairs={{80,112},{81,113},{82,114},{83,115},{84,116},{85,117},{86,118},{87... | collective-permute-start | bytes 786440 | tf_op jit(solution)/shard_map/far13/ppermute | solution.py:67
  364.7 3.7 collective-permute-start.41
  369.4 16.3 %collective-permute-start.42 = (f32[512,128]{1,0:T(8,128)S(1)}, f32[512,128]{1,0:T(8,128)S(1)}, u32[]{:S(2)}, u32[]{:S(2)}) collective-permute-start(f32[512,128]{1,0:T(8,128)S(1)} %fusion.1), channel_id=1, source_target_pairs={{96,112},{97,113},{98,114},{99,115},{100,116},{101,117},{102,118},... | collective-permute-start | bytes 786440 | tf_op jit(solution)/shard_map/near14/ppermute | solution.py:61
  (18 other events, 297.4 us)
Sparse Core Ops, SparseCore 0:
  82.6 59.5 all-gather.4
  144.0 92.3 all-gather.6

commit v2 on v1

v2 whole, which is shorter than its diff:
```python
import jax
import jax.numpy as jnp
from jax import lax
from jax.experimental import pallas as pl
from jax.experimental.pallas import tpu as pltpu
from jax.sharding import PartitionSpec as P

F32 = jnp.float32
BF16 = jnp.bfloat16
VMEM = pltpu.VMEM
SMEM = pltpu.SMEM
TILE = 128


def split(x):
    hi = x.astype(BF16)
    lo = (x - hi.astype(F32)).astype(BF16)
    return hi, lo


def left3(x):
    hi, lo = split(x)
    return jnp.concatenate([hi, hi, lo], 1)


def right3(x):
    hi, lo = split(x)
    return jnp.concatenate([hi, lo, hi], 0)


def dot3(a3, b3):
    return jnp.dot(a3, b3, preferred_element_type=F32)


def mm3(a, b):
    return dot3(left3(a), right3(b))


def vspec():
    return pl.BlockSpec(memory_space=VMEM)


def sspec():
    return pl.BlockSpec(memory_space=SMEM)


def aspec():
    return pl.BlockSpec(memory_space=pl.ANY)


PARAMS = pltpu.CompilerParams(vmem_limit_bytes=48 * 1024 * 1024)


def rows_loop(n, body):
    lax.fori_loop(0, n // TILE, lambda r, _: (body(pl.ds(pl.multiple_of(r * TILE, TILE), TILE)), 0)[1], 0)


def inverse_kernel(flag, own, out):
    nb = own.shape[1]
    h = nb // 2
    out[...] = own[...]

    def invert(slot):
        row = lax.broadcasted_iota(jnp.int32, (h, h), 0)
        col = lax.broadcasted_iota(jnp.int32, (h, h), 1)
        a0 = own[slot, :h, :h]
        a1 = own[slot, h:, h:]
        on = row == col
        y0 = jnp.where(on, 1.0 / jnp.where(on, a0, 1.0), 0.0)
        y1 = jnp.where(on, 1.0 / jnp.where(on, a1, 1.0), 0.0)

        def level(n, ys):
            y0, y1 = ys
            s = lax.shift_left(jnp.int32(1), n)
            pick = (lax.shift_right_logical(row, n + 1) == lax.shift_right_logical(col, n + 1))
            pick = pick & ((row & s) != 0) & ((col & s) == 0)
            e0 = jnp.where(pick, a0, 0.0)
            e1 = jnp.where(pick, a1, 0.0)
            z0 = mm3(e0, y0)
            z1 = mm3(e1, y1)
            return y0 - mm3(y0, z0), y1 - mm3(y1, z1)

        steps = h.bit_length() - 1
        y0, y1 = lax.fori_loop(0, steps, level, (y0, y1))
        z = mm3(own[slot, h:, :h], y0)
        out[slot, :h, :h] = y0
        out[slot, h:, h:] = y1
        out[slot, h:, :h] = -mm3(y1, z)
        out[slot, :h, h:] = jnp.zeros((h, h), F32)

    @pl.when(flag[0] > 0)
    def _():
        invert(flag[1])


def inverse_call(flag, own):
    return pl.pallas_call(
        inverse_kernel,
        out_shape=jax.ShapeDtypeStruct(own.shape, F32),
        in_specs=[sspec(), vspec()],
        out_specs=vspec(),
        compiler_params=PARAMS,
        name="inverse",
    )(flag, own)


def fetch(g, k, buf, sem):
    parts, _, rows, _ = g.shape
    return [
        pltpu.make_async_copy(g.at[a, k], buf.at[pl.ds(a * rows, rows)], sem.at[a])
        for a in range(parts)
    ]


def prep_kernel(idx, g, acc, inv3, near3, cur, b0, b1, s0, s1):
    c0 = fetch(g, idx[0], b0, s0)
    c1 = fetch(g, idx[1], b1, s1)
    for x in c0 + c1:
        x.start()
    for x in c0:
        x.wait()

    def put(ds):
        inv3[ds] = left3(b0[ds])

    rows_loop(b0.shape[0], put)
    for x in c1:
        x.wait()
    l3 = right3(b1[...])
    a3 = right3(acc[...])

    def mul(ds):
        near3[ds] = left3(dot3(inv3[ds], l3))
        cur[ds] = dot3(inv3[ds], a3)

    rows_loop(b0.shape[0], mul)


def prep_call(idx, g, acc):
    nb, width = acc.shape
    parts = g.shape[0]
    return pl.pallas_call(
        prep_kernel,
        out_shape=(
            jax.ShapeDtypeStruct((nb, 3 * nb), BF16),
            jax.ShapeDtypeStruct((nb, 3 * nb), BF16),
            jax.ShapeDtypeStruct((nb, width), F32),
        ),
        in_specs=[sspec(), aspec(), vspec()],
        out_specs=(vspec(), vspec(), vspec()),
        scratch_shapes=[
            VMEM((nb, nb), F32),
            VMEM((nb, nb), F32),
            pltpu.SemaphoreType.DMA((parts,)),
            pltpu.SemaphoreType.DMA((parts,)),
        ],
        compiler_params=PARAMS,
        name="prep",
    )(idx, g, acc)


def near_kernel(flag, near3, got, cur, mine, out):
    @pl.when(flag[0] > 0)
    def _():
        x3 = right3(got[...])

        def mul(ds):
            out[ds] = cur[ds] - dot3(near3[ds], x3)

        rows_loop(out.shape[0], mul)

    @pl.when(flag[0] == 0)
    def _():
        out[...] = mine[...]


def near_call(flag, near3, got, cur, mine):
    return pl.pallas_call(
        near_kernel,
        out_shape=jax.ShapeDtypeStruct(mine.shape, F32),
        in_specs=[sspec(), vspec(), vspec(), vspec(), vspec()],
        out_specs=vspec(),
        compiler_params=PARAMS,
        name="near",
    )(flag, near3, got, cur, mine)


def far_kernel(idx, g, inv3, acc, xb, xa, acc_out, cur_out, b0, b1, s0, s1):
    @pl.when(idx[2] > 0)
    def _():
        c0 = fetch(g, idx[0], b0, s0)
        c1 = fetch(g, idx[1], b1, s1)
        for x in c0 + c1:
            x.start()
        xb3 = right3(xb[...])
        xa3 = right3(xa[...])
        for x in c0 + c1:
            x.wait()

        def mul(ds):
            acc_out[ds] = acc[ds] - (dot3(left3(b0[ds]), xb3) + dot3(left3(b1[ds]), xa3))

        rows_loop(acc.shape[0], mul)
        a3 = right3(acc_out[...])

        def mul2(ds):
            cur_out[ds] = dot3(inv3[ds], a3)

        rows_loop(acc.shape[0], mul2)

    @pl.when(idx[2] == 0)
    def _():
        acc_out[...] = acc[...]
        cur_out[...] = acc[...]


def far_call(idx, g, inv3, acc, xb, xa):
    nb = acc.shape[0]
    parts = g.shape[0]
    return pl.pallas_call(
        far_kernel,
        out_shape=(
            jax.ShapeDtypeStruct(acc.shape, F32),
            jax.ShapeDtypeStruct(acc.shape, F32),
        ),
        in_specs=[sspec(), aspec(), vspec(), vspec(), vspec(), vspec()],
        out_specs=(vspec(), vspec()),
        scratch_shapes=[
            VMEM((nb, nb), F32),
            VMEM((nb, nb), F32),
            pltpu.SemaphoreType.DMA((parts,)),
            pltpu.SemaphoreType.DMA((parts,)),
        ],
        compiler_params=PARAMS,
        name="far",
    )(idx, g, inv3, acc, xb, xa)


def bulk_kernel(g, store, acc, out):
    k = pl.program_id(0)

    @pl.when(k == 0)
    def _():
        out[...] = acc[...]

    x3 = right3(store[0])

    def mul(ds):
        out[ds] = out[ds] - dot3(left3(g[0, 0, ds]), x3)

    rows_loop(out.shape[0], mul)


def bulk_call(g, store, acc, count):
    nb, width = acc.shape
    return pl.pallas_call(
        bulk_kernel,
        out_shape=jax.ShapeDtypeStruct(acc.shape, F32),
        grid=(count,),
        in_specs=[
            pl.BlockSpec((1, 1, nb, nb), lambda k: (0, k, 0, 0)),
            pl.BlockSpec((1, nb, width), lambda k: (k, 0, 0)),
            pl.BlockSpec((nb, width), lambda k: (0, 0)),
        ],
        out_specs=pl.BlockSpec((nb, width), lambda k: (0, 0)),
        compiler_params=PARAMS,
        name="bulk",
    )(g, store, acc)


def on_device(tri_panels, rhs_rows):
    R = lax.axis_size("row")
    C = lax.axis_size("col")
    p = lax.axis_index("row")
    c = lax.axis_index("col")
    nb = tri_panels.shape[1]
    half = nb // 2
    blocks = tri_panels.shape[0] // nb
    sub = nb // C
    width = rhs_rows.shape[1] // C
    parted = rhs_rows.reshape(blocks, sub, rhs_rows.shape[1])
    state = lax.all_to_all(parted, "col", split_axis=2, concat_axis=1, tiled=True)

    own = tri_panels.reshape(blocks, nb, nb)
    flag = jnp.stack([(c % R == p).astype(jnp.int32), c // R])
    own = inverse_call(flag, own)
    top, low = own[0], own[1]

    moved = lax.ppermute(top[half:], "col", [(i, i + R) for i in range(R)])
    piece = jnp.where(c < R, top[:half], moved)
    g0 = lax.all_gather(piece, "col", axis=0, tiled=False).reshape(2, R, half, nb)
    g1 = lax.all_gather(low, "col", axis=0, tiled=False).reshape(1, C, nb, nb)

    def ints(*v):
        return jnp.stack([jnp.asarray(x, jnp.int32) for x in v])

    acc0, acc1 = state[0], state[1]
    inv0, near0, cur0 = prep_call(ints(p, jnp.maximum(p - 1, 0)), g0, acc0)
    zero = jnp.zeros((nb, width), F32)
    store = jnp.zeros((R + 1, nb, width), F32)
    mine = jnp.where(p == 0, cur0, zero)
    out0 = mine
    for t in range(C - 1):
        s = t % R
        with jax.named_scope(f"near{t}"):
            P1 = lax.ppermute(mine, "row", [(s, (s + 1) % R)])
        B = [((t - j) % R, (t + 2 + j) % R) for j in range(3) if t - j >= 0 and t + 2 + j < C]
        A = [((t - j) % R, (t + 1 + j) % R) for j in range(1, 4) if t - j >= 0 and t + 1 + j < C]
        with jax.named_scope(f"far{t}"):
            XB = lax.ppermute(mine, "row", B) if B else zero
            XA = lax.ppermute(mine, "row", A) if A else zero
        q = (p - t) % R
        i = t + q
        kA = i - 2 * q + 1
        kB = kA + 1
        inwin = (q >= 2) & (q <= 4)
        first = t + 1 < R
        fi = ints(
            jnp.clip(kB, 0, R - 1 if first else C - 1),
            jnp.clip(kA, 0, R - 1 if first else C - 1),
            inwin,
        )
        turn = ints(p == (t + 1) % R)
        if first:
            mine = near_call(turn, near0, P1, cur0, mine)
            out0 = mine
            if B:
                store = lax.dynamic_update_index_in_dim(store, XB, jnp.where(inwin & (kB >= 0), kB, R), 0)
            if A:
                store = lax.dynamic_update_index_in_dim(store, XA, jnp.where(inwin & (kA >= 0), kA, R), 0)
            store = lax.dynamic_update_index_in_dim(store, P1, jnp.where(p == t + 1, t, R), 0)
            if t + 1 < R - 1:
                acc0, cur0 = far_call(fi, g0, inv0, acc0, XB, XA)
            else:
                store = lax.dynamic_update_index_in_dim(store, mine, p, 0)
                acc1 = bulk_call(g1, store, acc1, R)
                inv1, near1, cur1 = prep_call(ints(R + p, R + p - 1), g1, acc1)
        else:
            mine = near_call(turn, near1, P1, cur1, mine)
            if B or A:
                acc1, cur1 = far_call(fi, g1, inv1, acc1, XB, XA)
    return jnp.concatenate([out0, mine], 0)


def solution(mesh):
    return jax.shard_map(
        on_device,
        mesh=mesh,
        in_specs=(P("row", "col"), P(("row", "col"), None)),
        out_specs=P("row", "col"),
        check_vma=False,
    )
```

time: 402 us -> 332 us (0.83); the launches traced: 395 us -> 330 us
  matrix products: 86.8 us -> 0 us
  Pallas kernels: 0 us -> 73.6 us
  other arithmetic: 46.1 us -> 5.5 us
  waiting for transfers between devices: 155 us -> 139 us
  local copies, waits for them, and re-layouts: 26.5 us -> 31.2 us
    dot_general x65 -> x0, matrix products: 79.1 us -> none  [mm(): return jnp.dot(a, b, precision=HI, preferred_element_type=jnp.float32)]
    pallas_call x0 -> x32, Pallas kernels: none -> 73.6 us  [the longest x13 37.3 us: far_call(): pl.pallas_call(far_kernel, out_shape=(jax.ShapeDtypeStruct(acc.shape, F32...]
    another operation x3 -> x16, other arithmetic: 41 us -> 1.21 us  [the longest x15 1.13 us: ints(): return jnp.stack([jnp.asarray(x, jnp.int32) for x in v])]
    unnamed x42 -> x44, local copies, waits for them, and re-layouts: 5.03 us -> 21.7 us
    ppermute x27, waiting for transfers between devices: 97.3 us -> 85.7 us  [the longest x14 78.9 us: on_device(): XB = lax.ppermute(mine, 'row', B) if B else zero]
    dynamic_slice x1 -> x0, local copies, waits for them, and re-layouts: 9.51 us -> none  [block0(): return lax.dynamic_index_in_dim(g0, k, 1, keepdims=False).reshape(nb, nb)]
    another operation x13 -> x0, local copies, waits for them, and re-layouts: 7.9 us -> none
    another operation x7 -> x0, matrix products: 7.75 us -> none  [on_device(): inv = jax.scipy.linalg.solve_triangular(diag, eye, lower=True)]
  transfers between devices with their start and end apart: 46 -> 46, of which waited for: 12 -> 10; matrix products, arithmetic and copies ran while one was open for 25% -> 5% of each run, Pallas kernels for 0% -> 22%
where the time goes in v2:
time: 332 us; the launch traced here: 330 us
  waiting for transfers between devices  139 us (42%)
  Pallas kernels  73.6 us (22%)
  starting transfers between devices  65.6 us (20%)
  local copies, waits for them, and re-layouts  31.2 us (9%)
  between operations  14.7 us (4%)
  other arithmetic  5.5 us (2%)
    ppermute x14, waiting for transfers between devices, on_device(): XB = lax.ppermute(mine, 'row', B) if B else zero  78.9 us
    pallas_call x13, Pallas kernels, far_call(): pl.pallas_call(far_kernel, out_shape=(jax.ShapeDtypeStruct(acc.shape, F32...  37.3 us
    all_gather x1, waiting for transfers between devices, on_device(): lax.all_gather(piece, 'col', axis=0, tiled=False).reshape(2, R, half, nb)  27.2 us
    unnamed x44, local copies, waits for them, and re-layouts  21.7 us
    ppermute x14, starting transfers between devices, on_device(): XB = lax.ppermute(mine, 'row', B) if B else zero  18.4 us
    ppermute x15, starting transfers between devices, on_device(): P1 = lax.ppermute(mine, 'row', [(s, (s + 1) % R)])  17.5 us
    ppermute x13, starting transfers between devices, on_device(): XA = lax.ppermute(mine, 'row', A) if A else zero  17.3 us
    pallas_call x15, Pallas kernels, near_call(): pl.pallas_call(near_kernel, out_shape=jax.ShapeDtypeStruct(mine.shape, F3...  16.8 us
  transfers between devices with their start and end apart: 46, of which 10 were waited for; matrix products, arithmetic and copies ran while one was open for 5% of the time, Pallas kernels for 22%

profile of v2, /device:TPU:120, one launch (start us, length us, event | category | flops | bytes accessed | tf_op | source)
XLA Modules:
  0.0 329.6 jit_solution(11645151350622837255)
XLA Ops:
  6.6 1.6 copy-done.4
  9.7 4.9 %collective-permute-start = (f32[256,512]{1,0:T(8,128)}, f32[256,512]{1,0:T(8,128)S(1)}, u32[]{:S(2)}, u32[]{:S(2)}) collective-permute-start(f32[256,512]{1,0:T(8,128)} %slice_bitcast_fusion), channel_id=1, source_target_pairs={{0,8},{1,9},{2,10},{3,11},{4,12},{5,13},{6,14},{7,15},{16,24},{17,... | collective-permute-start | bytes 1572872 | tf_op jit(solution)/shard_map/ppermute | solution.py:289
  14.7 11.4 %collective-permute-done = f32[256,512]{1,0:T(8,128)S(1)} collective-permute-done((f32[256,512]{1,0:T(8,128)}, f32[256,512]{1,0:T(8,128)S(1)}, u32[]{:S(2)}, u32[]{:S(2)}) %collective-permute-start) | collective-permute-done | bytes 524320 | tf_op jit(solution)/shard_map/ppermute | solution.py:289
  29.2 2.8 reshape.46
  32.0 7.4 %all-to-all-start = ((f32[16,1,8192]{2,1,0:T(1,128)}), f32[16,1,8192]{2,1,0:T(1,128)S(1)}, u32[]{:S(2)}, u32[]{:S(2)}) async-start(f32[16,1,8192]{2,1,0:T(1,128)} %reshape.46), calls=%async_computation | async-start | bytes 1048576 | tf_op jit(solution)/shard_map/all_to_all | solution.py:282
  39.9 14.5 %all-to-all-done = f32[16,1,8192]{2,1,0:T(1,128)S(1)} async-done(((f32[16,1,8192]{2,1,0:T(1,128)}), f32[16,1,8192]{2,1,0:T(1,128)S(1)}, u32[]{:S(2)}, u32[]{:S(2)}) %all-to-all-start) | async-done | bytes 524320 | tf_op jit(solution)/shard_map/all_to_all | solution.py:282
  55.0 1.9 reduce
  56.9 1.8 reshape.47
  60.3 27.2 %all-gather.6.cloned.1.call-done = f32[4096,512]{1,0:T(8,128)} async-done(((f32[256,512]{1,0:T(8,128)}), f32[4096,512]{1,0:T(8,128)}) %all-gather.6.cloned.1.call-update) | async-done | bytes 8388624 | tf_op jit(solution)/shard_map/all_gather | solution.py:291
  87.6 4.3 %prep.2 = (bf16[512,1536]{1,0:T(8,128)(2,1)S(1)}, bf16[512,1536]{1,0:T(8,128)(2,1)S(1)}, f32[512,128]{1,0:T(8,128)S(1)}) custom-call(s32[2]{0:T(128)S(1)} %pad_add_fusion.idx, f32[2,8,256,512]{3,2,1,0:T(8,128)} %bitcast.124, f32[512,128]{1,0:T(8,128)S(1)} %bitcast.111), custom_call_target="tpu_custom_call" | custom-call | tf_op jit(solution)/shard_map/prep/pallas_call | solution.py:142
  96.4 1.7 copy.12
  116.0 28.6 %collective-permute-done.11.xb = f32[512,128]{1,0:T(8,128)S(1)} collective-permute-done((f32[512,128]{1,0:T(8,128)S(1)}, f32[512,128]{1,0:T(8,128)S(1)}, u32[]{:S(2)}, u32[]{:S(2)}) %collective-permute-start.11) | collective-permute-done | bytes 262176 | tf_op jit(solution)/shard_map/far3/ppermute | solution.py:310
  144.7 6.8 %collective-permute-done.12.xa = f32[512,128]{1,0:T(8,128)S(1)} collective-permute-done((f32[512,128]{1,0:T(8,128)S(1)}, f32[512,128]{1,0:T(8,128)S(1)}, u32[]{:S(2)}, u32[]{:S(2)}) %collective-permute-start.12) | collective-permute-done | bytes 262176 | tf_op jit(solution)/shard_map/far3/ppermute | solution.py:311
  151.5 4.7 %far.16 = (f32[512,128]{1,0:T(8,128)S(1)}, f32[512,128]{1,0:T(8,128)S(1)}) custom-call(s32[3]{0:T(128)S(1)} %pad_add_fusion.5.idx, f32[2,8,256,512]{3,2,1,0:T(8,128)} %bitcast.128, bf16[512,1536]{1,0:T(8,128)(2,1)S(1)} %get-tuple-element.37.inv3, f32[512,128]{1,0:T(8,128)S(1)} %get-tuple-element.43.acc, f32[512,128]{1,0:T(8,128)S(1)} %collective-permute-done.11.xb, ...), custom_call_target="tpu_custom_call" | custom-call | tf_op jit(solution)/shard_map/far/pallas_call | solution.py:220
  159.5 23.2 %collective-permute-done.14.xb = f32[512,128]{1,0:T(8,128)S(1)} collective-permute-done((f32[512,128]{1,0:T(8,128)S(1)}, f32[512,128]{1,0:T(8,128)S(1)}, u32[]{:S(2)}, u32[]{:S(2)}) %collective-permute-start.14) | collective-permute-done | bytes 262176 | tf_op jit(solution)/shard_map/far4/ppermute | solution.py:310
  182.8 4.6 %far.17 = (f32[512,128]{1,0:T(8,128)S(1)}, f32[512,128]{1,0:T(8,128)S(1)}) custom-call(s32[3]{0:T(128)S(1)} %pad_add_fusion.6.idx, f32[2,8,256,512]{3,2,1,0:T(8,128)} %bitcast.129, bf16[512,1536]{1,0:T(8,128)(2,1)S(1)} %get-tuple-element.37.inv3, f32[512,128]{1,0:T(8,128)S(1)} %get-tuple-element.45.acc, f32[512,128]{1,0:T(8,128)S(1)} %collective-permute-done.14.xb, ...), custom_call_target="tpu_custom_call" | custom-call | tf_op jit(solution)/shard_map/far/pallas_call | solution.py:220
  190.1 14.5 %collective-permute-done.17.xb = f32[512,128]{1,0:T(8,128)S(1)} collective-permute-done((f32[512,128]{1,0:T(8,128)S(1)}, f32[512,128]{1,0:T(8,128)S(1)}, u32[]{:S(2)}, u32[]{:S(2)}) %collective-permute-start.17) | collective-permute-done | bytes 262176 | tf_op jit(solution)/shard_map/far5/ppermute | solution.py:310
  204.8 5.3 %far.18 = (f32[512,128]{1,0:T(8,128)}, f32[512,128]{1,0:T(8,128)S(1)}) custom-call(s32[3]{0:T(128)S(1)} %pad_add_fusion.7.idx, f32[2,8,256,512]{3,2,1,0:T(8,128)} %bitcast.130, bf16[512,1536]{1,0:T(8,128)(2,1)S(1)} %get-tuple-element.37.inv3, f32[512,128]{1,0:T(8,128)S(1)} %get-tuple-element.47.acc, f32[512,128]{1,0:T(8,128)S(1)} %collective-permute-done.17.xb, ...), custom_call_target="tpu_custom_call" | custom-call | tf_op jit(solution)/shard_map/far/pallas_call | solution.py:220
  211.2 2.0 collective-permute-start.23
  214.5 2.0 collective-permute-start.21
  216.6 1.4 copy-done
  218.0 1.7 copy-done.1
  219.7 10.4 %bulk.1.acc = f32[512,128]{1,0:T(8,128)S(1)} custom-call(f32[1,16,512,512]{3,2,1,0:T(8,128)} %bitcast.115, f32[9,512,128]{2,1,0:T(8,128)S(1)} %copy-done.1, f32[512,128]{1,0:T(8,128)S(1)} %bitcast.114), custom_call_target="tpu_custom_call" | custom-call | tf_op jit(solution)/shard_map/bulk/pallas_call | solution.py:256
  230.1 4.3 %prep.3 = (bf16[512,1536]{1,0:T(8,128)(2,1)S(1)}, bf16[512,1536]{1,0:T(8,128)(2,1)S(1)}, f32[512,128]{1,0:T(8,128)S(1)}) custom-call(s32[2]{0:T(128)S(1)} %pad_add_fusion.8.idx, f32[1,16,512,512]{3,2,1,0:T(8,128)} %bitcast.116, f32[512,128]{1,0:T(8,128)S(1)} %bulk.1.acc), custom_call_target="tpu_custom_call" | custom-call | tf_op jit(solution)/shard_map/prep/pallas_call | solution.py:142
  234.4 1.7 near.22.mine
  237.5 2.0 collective-permute-start.26
  239.5 2.0 collective-permute-start.27
  244.2 1.8 near.23.mine
  246.0 1.4 collective-permute-start.25
  247.4 2.0 collective-permute-start.29
  249.4 2.0 collective-permute-start.30
  254.2 1.7 near.24.mine
  255.9 1.4 collective-permute-start.28
  258.7 2.0 collective-permute-start.33
  263.5 1.8 near.25.mine
  265.2 1.4 collective-permute-start.31
  272.1 1.7 near.26.mine
  276.6 1.5 collective-permute-start.39
  278.1 6.7 %collective-permute-done.35.xb = f32[512,128]{1,0:T(8,128)} collective-permute-done((f32[512,128]{1,0:T(8,128)}, f32[512,128]{1,0:T(8,128)}, u32[]{:S(2)}, u32[]{:S(2)}) %collective-permute-start.35) | collective-permute-done | bytes 262176 | tf_op jit(solution)/shard_map/far11/ppermute | solution.py:310
  285.7 5.1 %far.23 = (f32[512,128]{1,0:T(8,128)S(1)}, f32[512,128]{1,0:T(8,128)S(1)}) custom-call(s32[3]{0:T(128)S(1)} %pad_add_fusion.13.idx, f32[1,16,512,512]{3,2,1,0:T(8,128)} %bitcast.121, bf16[512,1536]{1,0:T(8,128)(2,1)S(1)} %get-tuple-element.51.inv3, f32[512,128]{1,0:T(8,128)S(1)} %copy-done.15, f32[512,128]{1,0:T(8,128)} %collective-permute-done.35.xb, ...), custom_call_target="tpu_custom_call" | custom-call | tf_op jit(solution)/shard_map/far/pallas_call | solution.py:220
  291.5 1.8 near.27.mine
  293.3 1.4 collective-permute-start.37
  297.3 1.6 collective-permute-done.38.xb
  299.9 5.1 %far.24 = (f32[512,128]{1,0:T(8,128)S(1)}, f32[512,128]{1,0:T(8,128)S(1)}) custom-call(s32[3]{0:T(128)S(1)} %pad_add_fusion.14.idx, f32[1,16,512,512]{3,2,1,0:T(8,128)} %bitcast.122, bf16[512,1536]{1,0:T(8,128)(2,1)S(1)} %get-tuple-element.51.inv3, f32[512,128]{1,0:T(8,128)S(1)} %copy-done.17, f32[512,128]{1,0:T(8,128)} %collective-permute-done.38.xb, ...), custom_call_target="tpu_custom_call" | custom-call | tf_op jit(solution)/shard_map/far/pallas_call | solution.py:220
  305.7 1.7 near.28.mine
  308.8 4.2 %collective-permute-done.41.xb = f32[512,128]{1,0:T(8,128)} collective-permute-done((f32[512,128]{1,0:T(8,128)}, f32[512,128]{1,0:T(8,128)}, u32[]{:S(2)}, u32[]{:S(2)}) %collective-permute-start.41) | collective-permute-done | bytes 262176 | tf_op jit(solution)/shard_map/far13/ppermute | solution.py:310
  314.0 5.8 %far.25 = (f32[512,128]{1,0:T(8,128)}, f32[512,128]{1,0:T(8,128)S(1)}) custom-call(s32[3]{0:T(128)S(1)} %pad_add_fusion.15.idx, f32[1,16,512,512]{3,2,1,0:T(8,128)} %bitcast.123, bf16[512,1536]{1,0:T(8,128)(2,1)S(1)} %get-tuple-element.51.inv3, f32[512,128]{1,0:T(8,128)S(1)} %copy-done.9, f32[512,128]{1,0:T(8,128)} %collective-permute-done.41.xb, ...), custom_call_target="tpu_custom_call" | custom-call | tf_op jit(solution)/shard_map/far/pallas_call | solution.py:220
  319.8 2.1 near.29
  (173 shorter events, 66.3 us)
Async XLA Ops:
  6.5 81.0 %all-gather.6.cloned.1.call-start = ((), (), s32[]{:S(2)}) async-start(), calls=%async_computation.2 | async-start | bytes 8912896 | tf_op jit(solution)/shard_map/all_gather | solution.py:291
  9.7 16.4 %collective-permute-start = (f32[256,512]{1,0:T(8,128)}, f32[256,512]{1,0:T(8,128)S(1)}, u32[]{:S(2)}, u32[]{:S(2)}) collective-permute-start(f32[256,512]{1,0:T(8,128)} %slice_bitcast_fusion), channel_id=1, source_target_pairs={{0,8},{1,9},{2,10},{3,11},{4,12},{5,13},{6,14},{7,15},{16,24},{17,... | collective-permute-start | bytes 1572872 | tf_op jit(solution)/shard_map/ppermute | solution.py:289
  14.7 13.5 %copy-start.20 = (f32[64,2048]{1,0:T(8,128)S(1)}, f32[64,2048]{1,0:T(8,128)}, u32[]{:S(2)}) copy-start(f32[64,2048]{1,0:T(8,128)} %param.3) | copy-start | bytes 1572868
  27.0 191.0 %all-gather.4.cloned.1.call-start = ((), (), s32[]{:S(2)}) async-start(), calls=%async_computation.1 | async-start | bytes 17825792 | tf_op jit(solution)/shard_map/all_gather | solution.py:292
  32.0 22.4 %all-to-all-start = ((f32[16,1,8192]{2,1,0:T(1,128)}), f32[16,1,8192]{2,1,0:T(1,128)S(1)}, u32[]{:S(2)}, u32[]{:S(2)}) async-start(f32[16,1,8192]{2,1,0:T(1,128)} %reshape.46), calls=%async_computation | async-start | bytes 1048576 | tf_op jit(solution)/shard_map/all_to_all | solution.py:282
  93.2 9.0 %collective-permute-start.3 = (f32[512,128]{1,0:T(8,128)}, f32[512,128]{1,0:T(8,128)}, u32[]{:S(2)}, u32[]{:S(2)}) collective-permute-start(f32[512,128]{1,0:T(8,128)} %broadcast_select_fusion.mine), channel_id=1, source_target_pairs={{0,32},{1,33},{2,34},{3,35},{4,36},{5,37},{6,38},{7,39},{8,40},{9,... | collective-permute-start | bytes 786440 | tf_op jit(solution)/shard_map/far0/ppermute | solution.py:310
  94.6 3.6 %collective-permute-start.1 = (f32[512,128]{1,0:T(8,128)}, f32[512,128]{1,0:T(8,128)}, u32[]{:S(2)}, u32[]{:S(2)}) collective-permute-start(f32[512,128]{1,0:T(8,128)} %broadcast_select_fusion.mine), channel_id=1, source_target_pairs={{0,16},{1,17},{2,18},{3,19},{4,20},{5,21},{6,22},{7,23},{8,24},{9,... | collective-permute-start | bytes 786440 | tf_op jit(solution)/shard_map/near0/ppermute | solution.py:306
  100.2 7.4 %collective-permute-start.5 = (f32[512,128]{1,0:T(8,128)S(1)}, f32[512,128]{1,0:T(8,128)S(1)}, u32[]{:S(2)}, u32[]{:S(2)}) collective-permute-start(f32[512,128]{1,0:T(8,128)S(1)} %near.15.mine), channel_id=1, source_target_pairs={{16,48},{0,64},{17,49},{1,65},{18,50},{2,66},{19,51},{3,67},{20,52... | collective-permute-start | bytes 786440 | tf_op jit(solution)/shard_map/far1/ppermute | solution.py:310
  100.9 6.8 %collective-permute-start.6 = (f32[512,128]{1,0:T(8,128)S(1)}, f32[512,128]{1,0:T(8,128)S(1)}, u32[]{:S(2)}, u32[]{:S(2)}) collective-permute-start(f32[512,128]{1,0:T(8,128)S(1)} %near.15.mine), channel_id=1, source_target_pairs={{0,48},{1,49},{2,50},{3,51},{4,52},{5,53},{6,54},{7,55},{8,56},{9,... | collective-permute-start | bytes 786440 | tf_op jit(solution)/shard_map/far1/ppermute | solution.py:311
  101.6 3.9 %collective-permute-start.2 = (f32[512,128]{1,0:T(8,128)S(1)}, f32[512,128]{1,0:T(8,128)S(1)}, u32[]{:S(2)}, u32[]{:S(2)}) collective-permute-start(f32[512,128]{1,0:T(8,128)S(1)} %near.15.mine), channel_id=1, source_target_pairs={{16,32},{17,33},{18,34},{19,35},{20,36},{21,37},{22,38},{23,39},{2... | collective-permute-start | bytes 786440 | tf_op jit(solution)/shard_map/near1/ppermute | solution.py:306
  105.6 6.3 %collective-permute-start.8 = (f32[512,128]{1,0:T(8,128)S(1)}, f32[512,128]{1,0:T(8,128)S(1)}, u32[]{:S(2)}, u32[]{:S(2)}) collective-permute-start(f32[512,128]{1,0:T(8,128)S(1)} %near.16.mine), channel_id=1, source_target_pairs={{32,64},{16,80},{0,96},{33,65},{17,81},{1,97},{34,66},{18,82},{2,9... | collective-permute-start | bytes 786440 | tf_op jit(solution)/shard_map/far2/ppermute | solution.py:310
  106.3 5.7 %collective-permute-start.9 = (f32[512,128]{1,0:T(8,128)S(1)}, f32[512,128]{1,0:T(8,128)S(1)}, u32[]{:S(2)}, u32[]{:S(2)}) collective-permute-start(f32[512,128]{1,0:T(8,128)S(1)} %near.16.mine), channel_id=1, source_target_pairs={{16,64},{0,80},{17,65},{1,81},{18,66},{2,82},{19,67},{3,83},{20,68... | collective-permute-start | bytes 786440 | tf_op jit(solution)/shard_map/far2/ppermute | solution.py:311
  106.9 1.4 collective-permute-start.4
  108.6 36.0 %collective-permute-start.11 = (f32[512,128]{1,0:T(8,128)S(1)}, f32[512,128]{1,0:T(8,128)S(1)}, u32[]{:S(2)}, u32[]{:S(2)}) collective-permute-start(f32[512,128]{1,0:T(8,128)S(1)} %near.17.mine), channel_id=1, source_target_pairs={{48,80},{32,96},{16,112},{49,81},{33,97},{17,113},{50,82},{34,98},... | collective-permute-start | bytes 786440 | tf_op jit(solution)/shard_map/far3/ppermute | solution.py:310
  109.9 41.5 %collective-permute-start.12 = (f32[512,128]{1,0:T(8,128)S(1)}, f32[512,128]{1,0:T(8,128)S(1)}, u32[]{:S(2)}, u32[]{:S(2)}) collective-permute-start(f32[512,128]{1,0:T(8,128)S(1)} %near.17.mine), channel_id=1, source_target_pairs={{32,80},{16,96},{0,112},{33,81},{17,97},{1,113},{34,82},{18,98},{2... | collective-permute-start | bytes 786440 | tf_op jit(solution)/shard_map/far3/ppermute | solution.py:311
  111.2 1.4 collective-permute-start.7
  112.7 70.0 %collective-permute-start.14 = (f32[512,128]{1,0:T(8,128)S(1)}, f32[512,128]{1,0:T(8,128)S(1)}, u32[]{:S(2)}, u32[]{:S(2)}) collective-permute-start(f32[512,128]{1,0:T(8,128)S(1)} %near.18.mine), channel_id=1, source_target_pairs={{64,96},{48,112},{32,0},{65,97},{49,113},{33,1},{66,98},{50,114},{... | collective-permute-start | bytes 786440 | tf_op jit(solution)/shard_map/far4/ppermute | solution.py:310
  114.0 68.7 %collective-permute-start.15 = (f32[512,128]{1,0:T(8,128)S(1)}, f32[512,128]{1,0:T(8,128)S(1)}, u32[]{:S(2)}, u32[]{:S(2)}) collective-permute-start(f32[512,128]{1,0:T(8,128)S(1)} %near.18.mine), channel_id=1, source_target_pairs={{48,96},{32,112},{16,0},{49,97},{33,113},{17,1},{50,98},{34,114},{... | collective-permute-start | bytes 786440 | tf_op jit(solution)/shard_map/far4/ppermute | solution.py:311
  115.3 40.9 %collective-permute-start.10 = (f32[512,128]{1,0:T(8,128)S(1)}, f32[512,128]{1,0:T(8,128)S(1)}, u32[]{:S(2)}, u32[]{:S(2)}) collective-permute-start(f32[512,128]{1,0:T(8,128)S(1)} %near.18.mine), channel_id=1, source_target_pairs={{64,80},{65,81},{66,82},{67,83},{68,84},{69,85},{70,86},{71,87},{7... | collective-permute-start | bytes 786440 | tf_op jit(solution)/shard_map/near4/ppermute | solution.py:306
  156.3 48.4 %collective-permute-start.17 = (f32[512,128]{1,0:T(8,128)S(1)}, f32[512,128]{1,0:T(8,128)S(1)}, u32[]{:S(2)}, u32[]{:S(2)}) collective-permute-start(f32[512,128]{1,0:T(8,128)S(1)} %near.19.mine), channel_id=1, source_target_pairs={{80,112},{64,0},{48,16},{81,113},{65,1},{49,17},{82,114},{66,2},{5... | collective-permute-start | bytes 786440 | tf_op jit(solution)/shard_map/far5/ppermute | solution.py:310
  157.6 47.1 %collective-permute-start.18 = (f32[512,128]{1,0:T(8,128)S(1)}, f32[512,128]{1,0:T(8,128)S(1)}, u32[]{:S(2)}, u32[]{:S(2)}) collective-permute-start(f32[512,128]{1,0:T(8,128)S(1)} %near.19.mine), channel_id=1, source_target_pairs={{64,112},{48,0},{32,16},{65,113},{49,1},{33,17},{66,114},{50,2},{3... | collective-permute-start | bytes 786440 | tf_op jit(solution)/shard_map/far5/ppermute | solution.py:311
  158.9 28.5 %collective-permute-start.13 = (f32[512,128]{1,0:T(8,128)S(1)}, f32[512,128]{1,0:T(8,128)S(1)}, u32[]{:S(2)}, u32[]{:S(2)}) collective-permute-start(f32[512,128]{1,0:T(8,128)S(1)} %near.19.mine), channel_id=1, source_target_pairs={{80,96},{81,97},{82,98},{83,99},{84,100},{85,101},{86,102},{87,103... | collective-permute-start | bytes 786440 | tf_op jit(solution)/shard_map/near5/ppermute | solution.py:306
  187.4 22.6 %collective-permute-start.16 = (f32[512,128]{1,0:T(8,128)S(1)}, f32[512,128]{1,0:T(8,128)S(1)}, u32[]{:S(2)}, u32[]{:S(2)}) collective-permute-start(f32[512,128]{1,0:T(8,128)S(1)} %near.20.mine), channel_id=1, source_target_pairs={{96,112},{97,113},{98,114},{99,115},{100,116},{101,117},{102,118},... | collective-permute-start | bytes 786440 | tf_op jit(solution)/shard_map/near6/ppermute | solution.py:306
  188.7 27.7 %collective-permute-start.19 = (f32[512,128]{1,0:T(8,128)S(1)}, f32[512,128]{1,0:T(8,128)S(1)}, u32[]{:S(2)}, u32[]{:S(2)}) collective-permute-start(f32[512,128]{1,0:T(8,128)S(1)} %near.20.mine), channel_id=1, source_target_pairs={{96,0},{80,16},{64,32},{97,1},{81,17},{65,33},{98,2},{82,18},{66,3... | collective-permute-start | bytes 786440 | tf_op jit(solution)/shard_map/far6/ppermute | solution.py:310
  189.4 27.1 %collective-permute-start.20 = (f32[512,128]{1,0:T(8,128)S(1)}, f32[512,128]{1,0:T(8,128)S(1)}, u32[]{:S(2)}, u32[]{:S(2)}) collective-permute-start(f32[512,128]{1,0:T(8,128)S(1)} %near.20.mine), channel_id=1, source_target_pairs={{80,0},{64,16},{48,32},{81,1},{65,17},{49,33},{82,2},{66,18},{50,3... | collective-permute-start | bytes 786440 | tf_op jit(solution)/shard_map/far6/ppermute | solution.py:311
  210.1 7.9 %copy-start.5 = (f32[1,16,32,128]{3,2,1,0:T(8,128)S(1)}, f32[1,16,32,128]{3,2,1,0:T(8,128)}, u32[]{:S(2)}) copy-start(f32[1,16,32,128]{3,2,1,0:T(8,128)} %copy.12) | copy-start | bytes 786436
  211.2 30.3 %collective-permute-start.23 = (f32[512,128]{1,0:T(8,128)S(1)}, f32[512,128]{1,0:T(8,128)}, u32[]{:S(2)}, u32[]{:S(2)}) collective-permute-start(f32[512,128]{1,0:T(8,128)S(1)} %near.21.mine), channel_id=1, source_target_pairs={{112,16},{96,32},{80,48},{113,17},{97,33},{81,49},{114,18},{98,34}... | collective-permute-start | bytes 786440 | tf_op jit(solution)/shard_map/far7/ppermute | solution.py:310
  213.1 28.3 %collective-permute-start.24 = (f32[512,128]{1,0:T(8,128)S(1)}, f32[512,128]{1,0:T(8,128)}, u32[]{:S(2)}, u32[]{:S(2)}) collective-permute-start(f32[512,128]{1,0:T(8,128)S(1)} %near.21.mine), channel_id=1, source_target_pairs={{96,16},{80,32},{64,48},{97,17},{81,33},{65,49},{98,18},{82,34},{6... | collective-permute-start | bytes 786440 | tf_op jit(solution)/shard_map/far7/ppermute | solution.py:311
  214.5 19.9 %collective-permute-start.21 = (f32[512,128]{1,0:T(8,128)S(1)}, f32[512,128]{1,0:T(8,128)}, u32[]{:S(2)}, u32[]{:S(2)}) collective-permute-start(f32[512,128]{1,0:T(8,128)S(1)} %near.21.mine), channel_id=1, source_target_pairs={{112,0},{113,1},{114,2},{115,3},{116,4},{117,5},{118,6},{119,7},{1... | collective-permute-start | bytes 786440 | tf_op jit(solution)/shard_map/near7/ppermute | solution.py:306
  236.1 8.2 %collective-permute-start.22 = (f32[512,128]{1,0:T(8,128)}, f32[512,128]{1,0:T(8,128)}, u32[]{:S(2)}, u32[]{:S(2)}) collective-permute-start(f32[512,128]{1,0:T(8,128)} %near.22.mine), channel_id=1, source_target_pairs={{0,16},{1,17},{2,18},{3,19},{4,20},{5,21},{6,22},{7,23},{8,24},{9,... | collective-permute-start | bytes 786440 | tf_op jit(solution)/shard_map/near8/ppermute | solution.py:306
  237.5 13.9 %collective-permute-start.26 = (f32[512,128]{1,0:T(8,128)}, f32[512,128]{1,0:T(8,128)}, u32[]{:S(2)}, u32[]{:S(2)}) collective-permute-start(f32[512,128]{1,0:T(8,128)} %near.22.mine), channel_id=1, source_target_pairs={{0,32},{112,48},{96,64},{1,33},{113,49},{97,65},{2,34},{114,50},{9... | collective-permute-start | bytes 786440 | tf_op jit(solution)/shard_map/far8/ppermute | solution.py:310
  239.5 11.9 %collective-permute-start.27 = (f32[512,128]{1,0:T(8,128)}, f32[512,128]{1,0:T(8,128)}, u32[]{:S(2)}, u32[]{:S(2)}) collective-permute-start(f32[512,128]{1,0:T(8,128)} %near.22.mine), channel_id=1, source_target_pairs={{112,32},{96,48},{80,64},{113,33},{97,49},{81,65},{114,34},{98,50}... | collective-permute-start | bytes 786440 | tf_op jit(solution)/shard_map/far8/ppermute | solution.py:311
  246.0 8.2 %collective-permute-start.25 = (f32[512,128]{1,0:T(8,128)}, f32[512,128]{1,0:T(8,128)}, u32[]{:S(2)}, u32[]{:S(2)}) collective-permute-start(f32[512,128]{1,0:T(8,128)} %near.23.mine), channel_id=1, source_target_pairs={{16,32},{17,33},{18,34},{19,35},{20,36},{21,37},{22,38},{23,39},{2... | collective-permute-start | bytes 786440 | tf_op jit(solution)/shard_map/near9/ppermute | solution.py:306
  247.4 13.3 %collective-permute-start.29 = (f32[512,128]{1,0:T(8,128)}, f32[512,128]{1,0:T(8,128)}, u32[]{:S(2)}, u32[]{:S(2)}) collective-permute-start(f32[512,128]{1,0:T(8,128)} %near.23.mine), channel_id=1, source_target_pairs={{16,48},{0,64},{112,80},{17,49},{1,65},{113,81},{18,50},{2,66},{11... | collective-permute-start | bytes 786440 | tf_op jit(solution)/shard_map/far9/ppermute | solution.py:310
  249.4 11.3 %collective-permute-start.30 = (f32[512,128]{1,0:T(8,128)}, f32[512,128]{1,0:T(8,128)}, u32[]{:S(2)}, u32[]{:S(2)}) collective-permute-start(f32[512,128]{1,0:T(8,128)} %near.23.mine), channel_id=1, source_target_pairs={{0,48},{112,64},{96,80},{1,49},{113,65},{97,81},{2,50},{114,66},{9... | collective-permute-start | bytes 786440 | tf_op jit(solution)/shard_map/far9/ppermute | solution.py:311
  255.9 7.6 %collective-permute-start.28 = (f32[512,128]{1,0:T(8,128)}, f32[512,128]{1,0:T(8,128)}, u32[]{:S(2)}, u32[]{:S(2)}) collective-permute-start(f32[512,128]{1,0:T(8,128)} %near.24.mine), channel_id=1, source_target_pairs={{32,48},{33,49},{34,50},{35,51},{36,52},{37,53},{38,54},{39,55},{4... | collective-permute-start | bytes 786440 | tf_op jit(solution)/shard_map/near10/ppermute | solution.py:306
  257.4 11.9 %collective-permute-start.32 = (f32[512,128]{1,0:T(8,128)}, f32[512,128]{1,0:T(8,128)}, u32[]{:S(2)}, u32[]{:S(2)}) collective-permute-start(f32[512,128]{1,0:T(8,128)} %near.24.mine), channel_id=1, source_target_pairs={{32,64},{16,80},{0,96},{33,65},{17,81},{1,97},{34,66},{18,82},{2,9... | collective-permute-start | bytes 786440 | tf_op jit(solution)/shard_map/far10/ppermute | solution.py:310
  258.7 10.6 %collective-permute-start.33 = (f32[512,128]{1,0:T(8,128)}, f32[512,128]{1,0:T(8,128)}, u32[]{:S(2)}, u32[]{:S(2)}) collective-permute-start(f32[512,128]{1,0:T(8,128)} %near.24.mine), channel_id=1, source_target_pairs={{16,64},{0,80},{112,96},{17,65},{1,81},{113,97},{18,66},{2,82},{11... | collective-permute-start | bytes 786440 | tf_op jit(solution)/shard_map/far10/ppermute | solution.py:311
  265.2 6.8 %collective-permute-start.31 = (f32[512,128]{1,0:T(8,128)}, f32[512,128]{1,0:T(8,128)}, u32[]{:S(2)}, u32[]{:S(2)}) collective-permute-start(f32[512,128]{1,0:T(8,128)} %near.25.mine), channel_id=1, source_target_pairs={{48,64},{49,65},{50,66},{51,67},{52,68},{53,69},{54,70},{55,71},{5... | collective-permute-start | bytes 786440 | tf_op jit(solution)/shard_map/near11/ppermute | solution.py:306
  266.7 18.0 %collective-permute-start.35 = (f32[512,128]{1,0:T(8,128)}, f32[512,128]{1,0:T(8,128)}, u32[]{:S(2)}, u32[]{:S(2)}) collective-permute-start(f32[512,128]{1,0:T(8,128)} %near.25.mine), channel_id=1, source_target_pairs={{48,80},{32,96},{16,112},{49,81},{33,97},{17,113},{50,82},{34,98},... | collective-permute-start | bytes 786440 | tf_op jit(solution)/shard_map/far11/ppermute | solution.py:310
  268.0 16.8 %collective-permute-start.36 = (f32[512,128]{1,0:T(8,128)}, f32[512,128]{1,0:T(8,128)}, u32[]{:S(2)}, u32[]{:S(2)}) collective-permute-start(f32[512,128]{1,0:T(8,128)} %near.25.mine), channel_id=1, source_target_pairs={{32,80},{16,96},{0,112},{33,81},{17,97},{1,113},{34,82},{18,98},{2... | collective-permute-start | bytes 786440 | tf_op jit(solution)/shard_map/far11/ppermute | solution.py:311
  273.8 17.7 %collective-permute-start.34 = (f32[512,128]{1,0:T(8,128)}, f32[512,128]{1,0:T(8,128)}, u32[]{:S(2)}, u32[]{:S(2)}) collective-permute-start(f32[512,128]{1,0:T(8,128)} %near.26.mine), channel_id=1, source_target_pairs={{64,80},{65,81},{66,82},{67,83},{68,84},{69,85},{70,86},{71,87},{7... | collective-permute-start | bytes 786440 | tf_op jit(solution)/shard_map/near12/ppermute | solution.py:306
  275.3 23.6 %collective-permute-start.38 = (f32[512,128]{1,0:T(8,128)}, f32[512,128]{1,0:T(8,128)}, u32[]{:S(2)}, u32[]{:S(2)}) collective-permute-start(f32[512,128]{1,0:T(8,128)} %near.26.mine), channel_id=1, source_target_pairs={{64,96},{48,112},{65,97},{49,113},{66,98},{50,114},{67,99},{51,115... | collective-permute-start | bytes 786440 | tf_op jit(solution)/shard_map/far12/ppermute | solution.py:310
  276.6 22.4 %collective-permute-start.39 = (f32[512,128]{1,0:T(8,128)}, f32[512,128]{1,0:T(8,128)}, u32[]{:S(2)}, u32[]{:S(2)}) collective-permute-start(f32[512,128]{1,0:T(8,128)} %near.26.mine), channel_id=1, source_target_pairs={{48,96},{32,112},{49,97},{33,113},{50,98},{34,114},{51,99},{35,115... | collective-permute-start | bytes 786440 | tf_op jit(solution)/shard_map/far12/ppermute | solution.py:311
  293.3 12.4 %collective-permute-start.37 = (f32[512,128]{1,0:T(8,128)}, f32[512,128]{1,0:T(8,128)}, u32[]{:S(2)}, u32[]{:S(2)}) collective-permute-start(f32[512,128]{1,0:T(8,128)} %near.27.mine), channel_id=1, source_target_pairs={{80,96},{81,97},{82,98},{83,99},{84,100},{85,101},{86,102},{87,103... | collective-permute-start | bytes 786440 | tf_op jit(solution)/shard_map/near13/ppermute | solution.py:306
  294.7 18.3 %collective-permute-start.41 = (f32[512,128]{1,0:T(8,128)}, f32[512,128]{1,0:T(8,128)}, u32[]{:S(2)}, u32[]{:S(2)}) collective-permute-start(f32[512,128]{1,0:T(8,128)} %near.27.mine), channel_id=1, source_target_pairs={{80,112},{81,113},{82,114},{83,115},{84,116},{85,117},{86,118},{87... | collective-permute-start | bytes 786440 | tf_op jit(solution)/shard_map/far13/ppermute | solution.py:310
  296.0 17.1 %collective-permute-start.42 = (f32[512,128]{1,0:T(8,128)}, f32[512,128]{1,0:T(8,128)}, u32[]{:S(2)}, u32[]{:S(2)}) collective-permute-start(f32[512,128]{1,0:T(8,128)} %near.27.mine), channel_id=1, source_target_pairs={{64,112},{65,113},{66,114},{67,115},{68,116},{69,117},{70,118},{71... | collective-permute-start | bytes 786440 | tf_op jit(solution)/shard_map/far13/ppermute | solution.py:311
  307.4 12.4 %collective-permute-start.40 = (f32[512,128]{1,0:T(8,128)}, f32[512,128]{1,0:T(8,128)}, u32[]{:S(2)}, u32[]{:S(2)}) collective-permute-start(f32[512,128]{1,0:T(8,128)} %near.28.mine), channel_id=1, source_target_pairs={{96,112},{97,113},{98,114},{99,115},{100,116},{101,117},{102,118},... | collective-permute-start | bytes 786440 | tf_op jit(solution)/shard_map/near14/ppermute | solution.py:306
  (19 other events, 21.5 us)
Sparse Core Ops, SparseCore 0:
  27.1 60.3 all-gather.5
  89.3 92.1 all-gather.3
